TPU v7x, 256 devices: a whole 4x4x8 slice. The times are simulated.
256 devices in a mesh: row: 32 (over z_hi, x, y), col: 8 (over z_lo, core).
Axes of the slice: x: 4, y: 4, z: 8 (z_hi: 2, z_lo: 4; z = z_hi * 4 + z_lo), core: 2. Of those that a mesh axis runs over, the one named last changes fastest.
Arguments:
- query_proj: bfloat16 [768, 768, 128], P('row', 'col'), may hold values from -8 to 8
- key_proj: bfloat16 [768, 768, 128], P('row', 'col'), may hold values from -8 to 8
- value_proj: bfloat16 [768, 768, 128], P('row', 'col'), may hold values from -6 to 6
- pair_bias: bfloat16 [4, 768, 768], P(None, 'col', 'row'), may hold values from -9 to 9
- pair_mask: int32 [768, 768], P('row', 'col'), may hold values 0 or 1
- grad_out: bfloat16 [768, 768, 128], P('row', 'col'), may hold values from -18 to 18
Outputs:
- grad_query: bfloat16 [768, 768, 128], P('row', 'col')
- grad_key: bfloat16 [768, 768, 128], P('row', 'col')
- grad_value: bfloat16 [768, 768, 128], P('row', 'col')
- grad_bias: float32 [4, 768, 768], P(None, 'col', 'row')
All inputs are finite; a program needn't handle non-finite values. No bound on the sum of `pair_mask` on one device may be relied on, other than what follows from the above.
Results may differ from a plain program's by a relative error of at most 0.0096.
Values may be sent and summed in bfloat16 or wider, within the bound.
No kernel may reach another device: no remote copies, remote signals or barrier semaphores. Data moves between devices by JAX's collectives and lax.ppermute only.
A program may use at most 128 MiB of HBM per device.

v0:
```python
import math

import jax
import jax.numpy as jnp
from jax import lax
from jax.experimental import pallas as pl
from jax.experimental.pallas import tpu as pltpu
from jax.sharding import Mesh
from jax.sharding import PartitionSpec as P


HEADS = 4
HEAD_DIM = 32
LANES = 128
ROWS = ("zh", "x", "y")
COL = ("z", "core")
PLANE = ("x", "y")
COLUMN = ("zh", "z")
CHUNKS = ((0, 8), (8, 4))
GROUP = 4
FAR_FIRST = (6, 7, 4, 5, 2, 3, 1)
TILE = 256
BF16 = jnp.bfloat16
F32 = jnp.float32


def lane_slot(shape):
    return lax.broadcasted_iota(jnp.int32, shape, len(shape) - 1) // HEAD_DIM


def turned(value, slots):
    return pltpu.roll(value, (slots * HEAD_DIM) & (LANES - 1), value.ndim - 1)


def small_input():
    return pl.BlockSpec(memory_space=pltpu.SMEM)


def in_vmem(count):
    return [pl.BlockSpec(memory_space=pltpu.VMEM) for _ in range(count)]


def pack_body(place, *refs, with_mask):
    tensors = refs[:4]
    mask = refs[4] if with_mask else None
    outs = refs[-8:]
    z, core = place[0], place[1]
    rows, queries = tensors[0].shape[1], tensors[0].shape[2]
    slot = lane_slot((queries, LANES))

    def one_row(r, carry):
        for kc in range(2):
            half = core ^ kc
            parts = [t[half, r].astype(F32) for t in tensors]
            for kz in range(4):
                head = z ^ kz
                packed = turned(parts[0], 4 - head)
                for t in range(1, 4):
                    packed = jnp.where(slot == t, turned(parts[t], 4 + t - head), packed)
                start = pl.multiple_of(r * queries, 16)
                outs[kz * 2 + kc][pl.ds(start, queries), :] = packed.astype(BF16)
        return carry

    lax.fori_loop(0, rows, one_row, 0)
    if with_mask:
        for kc in range(2):
            count = mask.shape[0] // 2
            present = jnp.where((core ^ kc) == 0, mask[:count, :], mask[count:, :]).astype(F32)
            present = jnp.concatenate([present, jnp.zeros((16 - count, queries), F32)], axis=0)
            for kz in range(4):
                outs[kz * 2 + kc][rows * queries :, :queries] = present.astype(BF16)
                outs[kz * 2 + kc][rows * queries :, queries:] = jnp.zeros((16, LANES - queries), BF16)


def pack(place, tensors, mask, chunk):
    halves, _, queries, _ = tensors[0].shape
    first_row, rows = CHUNKS[chunk]
    length = rows * queries + (0 if mask is None else 16)
    block = pl.BlockSpec((halves, rows, queries, LANES), lambda i: (0, first_row // rows, 0, 0))
    operands = list(tensors)
    specs = [block] * 4
    if mask is not None:
        operands.append(mask)
        specs.append(pl.BlockSpec(mask.shape, lambda i: (0, 0)))
    return pl.pallas_call(
        lambda *refs: pack_body(*refs, with_mask=mask is not None),
        grid=(1,),
        in_specs=[small_input()] + specs,
        out_specs=[pl.BlockSpec((length, LANES), lambda i: (0, 0))] * 8,
        out_shape=[jax.ShapeDtypeStruct((length, LANES), BF16)] * 8,
        cost_estimate=pl.CostEstimate(flops=10**9, bytes_accessed=2 * 10**6, transcendentals=0),
    )(place, *operands)


def position(place, k):
    return (k & 1) * 4 + (place[0] ^ (k >> 1))


def attention_body(place, *refs, first_row, rows):
    first = first_row == 0
    tiles = refs[:8]
    bias = refs[8]
    if first:
        (outs, bias_grad, mask_out), scratch = (refs[9:17], refs[17], refs[18]), refs[19:]
        mask_lanes = mask_out
    else:
        mask_lanes, bias_grad_in = refs[9], refs[10]
        (outs, bias_grad), scratch = (refs[11:19], refs[19]), refs[20:]
    pairs, probs, scores_low, logits, grad_probs, key_sum, value_sum, query_sum, masked = scratch
    length = pairs.shape[0]
    block = length // 8
    strip = block
    scale = 1.0 / math.sqrt(HEAD_DIM)

    if first:
        bias_grad[...] = jnp.zeros_like(bias_grad)
        pick = (
            lax.broadcasted_iota(jnp.int32, (16, LANES), 0)
            == lax.broadcasted_iota(jnp.int32, (16, LANES), 1)
        ).astype(BF16)
        for k in range(8):
            start = pl.multiple_of(position(place, k) * block, 16)
            columns = lax.dot_general(
                tiles[k][rows * block :, :], pick, (((0,), (0,)), ((), ())), preferred_element_type=F32
            )
            mask_out[pl.ds(start, block), :] = columns[:block].astype(BF16)
    else:
        bias_grad[...] = bias_grad_in[...]
    key_sum[...] = jnp.zeros_like(key_sum)
    value_sum[...] = jnp.zeros_like(value_sum)
    groups = rows // GROUP

    def one_row(r, carry):
        for k in range(8):
            start = pl.multiple_of(position(place, k) * block, 16)
            source = pl.multiple_of(r * block, 16)
            pairs[pl.ds(start, block), :] = tiles[k][pl.ds(source, block), :]
        slot = lane_slot((length, LANES))
        wide = pairs[...].astype(F32)
        zero = jnp.zeros_like(wide)
        query_at_key = jnp.where(slot == 1, pltpu.roll(wide, HEAD_DIM, 1), zero).astype(BF16)
        grad_at_value = jnp.where(slot == 2, pltpu.roll(wide, LANES - HEAD_DIM, 1), zero).astype(BF16)
        group, in_group = r // GROUP, r % GROUP
        query_at_row = jnp.where(slot == in_group, turned(wide, in_group), zero).astype(BF16)
        grad_at_row = jnp.where(slot == in_group, turned(wide, in_group + 1), zero).astype(BF16)
        keys_turned = jnp.transpose(wide)[HEAD_DIM : 2 * HEAD_DIM, :].astype(BF16)
        chosen = (lax.broadcasted_iota(jnp.int32, (LANES, LANES), 0) == r + first_row).astype(BF16)
        masked[...] = 1000000000.0 * (
            jnp.dot(mask_lanes[...], chosen, preferred_element_type=F32) - 1.0
        )
        for j in range(0, length, TILE):
            right_query = query_at_key[j : j + TILE]
            right_grad = grad_at_value[j : j + TILE]
            top = jnp.full((8, TILE), -jnp.inf, F32)
            for i in range(0, length, strip):
                s = lax.dot_general(
                    pairs[i : i + strip, :],
                    right_query,
                    (((1,), (1,)), ((), ())),
                    preferred_element_type=F32,
                )
                mask_strip = masked[i : i + strip, :]
                t = (
                    s * scale
                    + bias[i : i + strip, j : j + TILE]
                    + jnp.concatenate([mask_strip] * (TILE // LANES), axis=1)
                )
                logits[i : i + strip, :] = t
                top = jnp.maximum(top, jnp.max(t.reshape(strip // 8, 8, TILE), axis=0))
            top = jnp.max(top, axis=0, keepdims=True)
            total = jnp.zeros((8, TILE), F32)
            delta = jnp.zeros((8, TILE), F32)
            for i in range(0, length, strip):
                gp = lax.dot_general(
                    pairs[i : i + strip, :],
                    right_grad,
                    (((1,), (1,)), ((), ())),
                    preferred_element_type=F32,
                )
                e = jnp.exp(logits[i : i + strip, :] - top)
                logits[i : i + strip, :] = e
                grad_probs[i : i + strip, :] = gp
                total = total + jnp.sum(e.reshape(strip // 8, 8, TILE), axis=0)
                delta = delta + jnp.sum((e * gp).reshape(strip // 8, 8, TILE), axis=0)
            inverse = 1.0 / jnp.sum(total, axis=0, keepdims=True)
            delta = jnp.sum(delta, axis=0, keepdims=True) * inverse
            for i in range(0, length, strip):
                p = logits[i : i + strip, :] * inverse
                ds = p * (grad_probs[i : i + strip, :] - delta)
                probs[i : i + strip, j : j + TILE] = p.astype(BF16)
                scores_low[i : i + strip, j : j + TILE] = ds.astype(BF16)
                bias_grad[i : i + strip, j : j + TILE] += ds
        value_sum[group] += jnp.dot(probs[...], grad_at_row, preferred_element_type=F32)
        key_sum[group] += jnp.dot(scores_low[...], query_at_row, preferred_element_type=F32)
        query_sum[pl.ds(pl.multiple_of(r * HEAD_DIM, 32), HEAD_DIM), :] = jnp.dot(
            keys_turned, scores_low[...], preferred_element_type=F32
        )
        return carry

    lax.fori_loop(0, rows, one_row, 0)
    for g in range(groups):
        lanes = pl.ds(g * LANES, LANES)
        probs[:, lanes] = (jnp.transpose(query_sum[lanes, :]) * scale).astype(BF16)
        scores_low[:, lanes] = (key_sum[g] * scale).astype(BF16)
        scores_low[:, pl.ds((groups + g) * LANES, LANES)] = value_sum[g].astype(BF16)
    for k in range(8):
        start = pl.multiple_of(position(place, k) * block, 16)
        for g in range(3 * groups):
            held, lane = (probs, g) if g < groups else (scores_low, g - groups)
            outs[k][g * block : (g + 1) * block, :] = held[
                pl.ds(start, block), lane * LANES : (lane + 1) * LANES
            ]


def attention(place, tiles, bias, mask_lanes, bias_grad, chunk):
    first = chunk == 0
    first_row, rows = CHUNKS[chunk]
    groups = rows // GROUP
    length = bias.shape[0]
    block = length // 8
    operands = [*tiles, bias]
    if not first:
        operands += [mask_lanes, bias_grad]
    out_shape = [jax.ShapeDtypeStruct((3 * groups * block, LANES), BF16)] * 8
    out_shape.append(jax.ShapeDtypeStruct((length, length), F32))
    if first:
        out_shape.append(jax.ShapeDtypeStruct((length, LANES), BF16))
    results = pl.pallas_call(
        lambda *refs: attention_body(*refs, first_row=first_row, rows=rows),
        in_specs=[small_input()] + in_vmem(len(operands)),
        out_specs=in_vmem(len(out_shape)),
        out_shape=out_shape,
        scratch_shapes=[
            pltpu.VMEM((length, LANES), BF16),
            pltpu.VMEM((length, length), BF16),
            pltpu.VMEM((length, length), BF16),
            pltpu.VMEM((length, TILE), F32),
            pltpu.VMEM((length, TILE), F32),
            pltpu.VMEM((groups, length, LANES), F32),
            pltpu.VMEM((groups, length, LANES), F32),
            pltpu.VMEM((groups * LANES, length), F32),
            pltpu.VMEM((length, LANES), F32),
        ],
        input_output_aliases={} if first else {len(operands): 8},
        cost_estimate=pl.CostEstimate(
            flops=10**10, bytes_accessed=6 * 10**6, transcendentals=length * length * rows
        ),
        compiler_params=pltpu.CompilerParams(vmem_limit_bytes=40 * 2**20),
    )(place, *operands)
    if first:
        return results[:8], results[8], results[9]
    return results[:8], results[8], mask_lanes


def unpack_body(place, *refs):
    parts = refs[:8]
    outs = refs[-3:]
    z, core = place[0], place[1]
    rows, queries = outs[0].shape[1], outs[0].shape[2]
    groups = rows // GROUP
    slot = lane_slot((queries, LANES))
    for kc in range(2):
        half = core ^ kc
        for g in range(3 * groups):
            heads = [parts[kz * 2 + kc][g * queries : (g + 1) * queries, :].astype(F32) for kz in range(4)]
            for r in range(GROUP):
                row = turned(heads[0], 4 + z - r)
                for kz in range(1, 4):
                    head = z ^ kz
                    row = jnp.where(slot == head, turned(heads[kz], 4 + head - r), row)
                outs[g // groups][half, g % groups * GROUP + r] = row.astype(BF16)


def unpack(place, parts, outs, chunk, shape):
    first = outs is None
    halves, _, queries, lanes = shape
    first_row, rows = CHUNKS[chunk]
    block = pl.BlockSpec((halves, rows, queries, lanes), lambda i: (0, first_row // rows, 0, 0))
    piece = pl.BlockSpec(parts[0].shape, lambda i: (0, 0))
    kept = [] if first else list(outs)
    return pl.pallas_call(
        lambda *refs: unpack_body(*refs),
        grid=(1,),
        in_specs=[small_input()] + [piece] * 8 + [pl.BlockSpec(memory_space=pl.ANY)] * len(kept),
        out_specs=[block] * 3,
        out_shape=[jax.ShapeDtypeStruct(shape, BF16)] * 3,
        input_output_aliases={} if first else {9: 0, 10: 1, 11: 2},
    )(place, *parts, *kept)


def bias_rows(place, length):
    block = length // 8
    for zh in range(2):
        for x in range(4):
            tile = zh * 4 + x
            start = (((tile & 1) ^ place[1]) * 4 + (tile >> 1)) * block
            for y in range(4):
                part = block // 4
                yield x * 4 + y, zh * part, part, pl.multiple_of(start + y * part, 8)


def bias_in_body(place, own, other, out):
    length = out.shape[0]
    half = length // 2
    for row, line, part, start in bias_rows(place, length):
        out[pl.ds(start, part), :half] = own[row, line : line + part, :].astype(F32)
        out[pl.ds(start, part), half:] = other[row, line : line + part, :].astype(F32)


def bias_out_body(place, whole, own, other):
    length = whole.shape[0]
    half = length // 2
    for row, line, part, start in bias_rows(place, length):
        own[row, line : line + part, :] = whole[pl.ds(start, part), :half]
        other[row, line : line + part, :] = whole[pl.ds(start, part), half:].astype(BF16)


def swapped(value, k, axes):
    count = lax.axis_size(axes)
    return lax.ppermute(value, axes, [(i, i ^ k) for i in range(count)])


def sent(values):
    arrived = dict.fromkeys(range(8))
    arrived[0] = values[0]
    for k in FAR_FIRST:
        arrived[k] = swapped(values[k], k, COL)
    return list(arrived.values())


def exchanged(value, axes):
    return lax.all_to_all(value, axes, split_axis=0, concat_axis=0, tiled=True)


def gathered_bias(place, pair_bias):
    heads, queries, keys = pair_bias.shape
    turned_bias = jnp.transpose(pair_bias, (0, 2, 1))
    both = jnp.concatenate([turned_bias] * 2, axis=0)
    column = exchanged(both, COLUMN)
    lines = jnp.transpose(column.reshape(2, heads, keys, queries), (0, 2, 1, 3))
    lines = lines.reshape(2 * keys, heads * queries)
    own = exchanged(jnp.broadcast_to(lines, (16, *lines.shape)), PLANE)
    other = swapped(own, 1, "core")
    length = 8 * queries
    return pl.pallas_call(
        bias_in_body,
        in_specs=[small_input()] + in_vmem(2),
        out_specs=in_vmem(1)[0],
        out_shape=jax.ShapeDtypeStruct((length, length), F32),
        compiler_params=pltpu.CompilerParams(vmem_limit_bytes=16 * 2**20),
        name="bias_in",
    )(place, own, other)


def reduced_bias(place, bias_grad, heads):
    length = bias_grad.shape[0]
    queries = length // 8
    keys = length // 32
    shape = (16, 2 * keys, length // 2)
    own, other = pl.pallas_call(
        bias_out_body,
        in_specs=[small_input()] + in_vmem(1),
        out_specs=in_vmem(2),
        out_shape=[jax.ShapeDtypeStruct(shape, F32), jax.ShapeDtypeStruct(shape, BF16)],
        compiler_params=pltpu.CompilerParams(vmem_limit_bytes=16 * 2**20),
        name="bias_out",
    )(place, bias_grad)
    own = (own + swapped(other, 1, "core").astype(F32)).astype(BF16)
    lines = jnp.sum(exchanged(own, PLANE).astype(F32), axis=0).astype(BF16)
    lines = jnp.transpose(lines.reshape(2, keys, heads, queries), (0, 2, 1, 3))
    column = exchanged(lines.reshape(2 * heads, keys, queries), COLUMN)
    column = jnp.sum(column.astype(F32).reshape(2, heads, keys, queries), axis=0)
    return jnp.transpose(column, (0, 2, 1))


def all_rows(query_proj, key_proj, value_proj, pair_bias, pair_mask, grad_out):
    row_count, queries, lanes = query_proj.shape
    shape = (2, row_count // 2, queries, lanes)
    place = jnp.stack([lax.axis_index("z"), lax.axis_index("core")]).astype(jnp.int32)
    tensors = [t.reshape(shape) for t in (query_proj, key_proj, value_proj, grad_out)]
    bias = gathered_bias(place, pair_bias)
    chunks = range(len(CHUNKS))
    arrived = []
    for chunk in chunks:
        packed = pack(place, tensors, pair_mask if chunk == 0 else None, chunk)
        arrived.append(sent(packed))
    outs = mask_lanes = bias_grad = None
    returned = []
    for chunk in chunks:
        grads, bias_grad, mask_lanes = attention(place, arrived[chunk], bias, mask_lanes, bias_grad, chunk)
        returned.append(sent(grads))
    grad_bias = reduced_bias(place, bias_grad, HEADS)
    for chunk in chunks:
        outs = unpack(place, returned[chunk], outs, chunk, shape)
    grads = [o.reshape(query_proj.shape) for o in outs]
    return (*grads, grad_bias)


def solution(mesh):
    torus = Mesh(mesh.devices.reshape(2, 4, 4, 4, 2), ("zh", "x", "y", "z", "core"))
    placed = (
        P(ROWS, COL, None),
        P(ROWS, COL, None),
        P(ROWS, COL, None),
        P(None, COL, ROWS),
        P(ROWS, COL),
        P(ROWS, COL, None),
    )
    return jax.shard_map(
        all_rows,
        mesh=torus,
        in_specs=placed,
        out_specs=(P(ROWS, COL, None), P(ROWS, COL, None), P(ROWS, COL, None), P(None, COL, ROWS)),
        check_vma=False,
    )
```

profile of v0, /device:TPU:38, one launch (start us, length us, event | category | flops | bytes accessed | tf_op | source)
XLA Modules:
  0.0 196.1 jit_solution(2688666412478724141)
XLA Ops:
  1.5 15.1 %all_to_all.20 = bf16[8,24,96]{2,1,0:T(8,128)(2,1)S(1)} all-to-all(bf16[8,24,96]{2,1,0:T(8,128)(2,1)S(1)} %pad_maximum_fusion), channel_id=1, replica_groups=mesh['zh'=2,'x'=4,'y'=4,'z'=4,'core'=2] {'zh','z'}, dimensions={0} | all-to-all | bytes 73728 | tf_op jit(solution)/shard_map/all_to_all | solution.py:332
  16.8 16.0 %all_to_all.21.own = bf16[16,48,384]{2,1,0:T(8,128)(2,1)S(1)} all-to-all(bf16[16,48,384]{2,1,0:T(8,128)(2,1)S(1)} %broadcast_in_dim.3), channel_id=1, replica_groups=mesh['zh'=2,'x'=4,'y'=4,'z'=4,'core'=2] {'x','y'}, dimensions={0} | all-to-all | bytes 1179648 | tf_op jit(solution)/shard_map/all_to_all | solution.py:332
  33.4 4.7 %shard_map.94 = (bf16[784,128]{1,0:T(8,128)(2,1)}, bf16[784,128]{1,0:T(8,128)(2,1)}, bf16[784,128]{1,0:T(8,128)(2,1)}, bf16[784,128]{1,0:T(8,128)(2,1)}, bf16[78...) custom-call(s32[2]{0:T(128)} %pad_add_fusion.refs_0_.place, ...), custom_call_target="tpu_custom_call" | custom-call | flops 1000000000 | bytes 2000000 | tf_op jit(solution)/shard_map/pallas_call | solution.py:85
  38.7 1.5 collective-permute-start.9
  40.2 3.2 %shard_map.93 = (bf16[384,128]{1,0:T(8,128)(2,1)}, bf16[384,128]{1,0:T(8,128)(2,1)}, bf16[384,128]{1,0:T(8,128)(2,1)}, bf16[384,128]{1,0:T(8,128)(2,1)}, bf16[38...) custom-call(s32[2]{0:T(128)} %pad_add_fusion.refs_0_.place, ...), custom_call_target="tpu_custom_call" | custom-call | flops 1000000000 | bytes 2000000 | tf_op jit(solution)/shard_map/pallas_call | solution.py:85
  45.2 4.1 %collective-permute-done.1.refs_3_ = bf16[384,128]{1,0:T(8,128)(2,1)S(1)} collective-permute-done((bf16[384,128]{1,0:T(8,128)(2,1)}, bf16[384,128]{1,0:T(8,128)(2,1)S(1)}, u32[]{:S(2)}, u32[]{:S(2)}) %collective-permute-start.1) | collective-permute-done | bytes 98336 | tf_op jit(solution)/shard_map/ppermute | solution.py:320
  51.5 2.3 %collective-permute-start.14 = (bf16[784,128]{1,0:T(8,128)(2,1)S(1)}, bf16[784,128]{1,0:T(8,128)(2,1)S(1)}, u32[]{:S(2)}, u32[]{:S(2)}) collective-permute-start(bf16[784,128]{1,0:T(8,128)(2,1)S(1)} %copy-done.19), channel_id=1, source_target_pairs={{0,7},{1,6},{2,5},{3,4},{4,3},{5,2},{6,1},{7,0},{8,15},{9,14},{10,... | collective-permute-start | bytes 602120 | tf_op jit(solution)/shard_map/ppermute | solution.py:320
  54.6 1.3 collective-permute-start.2
  55.9 15.8 %collective-permute-done.11.refs_5_ = bf16[784,128]{1,0:T(8,128)(2,1)S(1)} collective-permute-done((bf16[784,128]{1,0:T(8,128)(2,1)S(1)}, bf16[784,128]{1,0:T(8,128)(2,1)S(1)}, u32[]{:S(2)}, u32[]{:S(2)}) %collective-permute-start.11) | collective-permute-done | bytes 200736 | tf_op jit(solution)/shard_map/ppermute | solution.py:320
  71.7 3.4 %collective-permute-start.3 = (bf16[384,128]{1,0:T(8,128)(2,1)S(1)}, bf16[384,128]{1,0:T(8,128)(2,1)S(1)}, u32[]{:S(2)}, u32[]{:S(2)}) collective-permute-start(bf16[384,128]{1,0:T(8,128)(2,1)S(1)} %copy-done.27), channel_id=1, source_target_pairs={{0,4},{1,5},{2,6},{3,7},{4,0},{5,1},{6,2},{7,3},{8,12},{9,13},{10,... | collective-permute-start | bytes 294920 | tf_op jit(solution)/shard_map/ppermute | solution.py:320
  75.1 2.0 %collective-permute-done.12.refs_6_ = bf16[784,128]{1,0:T(8,128)(2,1)S(1)} collective-permute-done((bf16[784,128]{1,0:T(8,128)(2,1)S(1)}, bf16[784,128]{1,0:T(8,128)(2,1)S(1)}, u32[]{:S(2)}, u32[]{:S(2)}) %collective-permute-start.12) | collective-permute-done | bytes 200736 | tf_op jit(solution)/shard_map/ppermute | solution.py:320
  77.1 3.8 %collective-permute-start.4 = (bf16[384,128]{1,0:T(8,128)(2,1)S(1)}, bf16[384,128]{1,0:T(8,128)(2,1)S(1)}, u32[]{:S(2)}, u32[]{:S(2)}) collective-permute-start(bf16[384,128]{1,0:T(8,128)(2,1)S(1)} %copy-done.26), channel_id=1, source_target_pairs={{0,5},{1,4},{2,7},{3,6},{4,1},{5,0},{6,3},{7,2},{8,13},{9,12},{10,... | collective-permute-start | bytes 294920 | tf_op jit(solution)/shard_map/ppermute | solution.py:320
  80.9 9.9 %collective-permute-done.13.refs_7_ = bf16[784,128]{1,0:T(8,128)(2,1)S(1)} collective-permute-done((bf16[784,128]{1,0:T(8,128)(2,1)S(1)}, bf16[784,128]{1,0:T(8,128)(2,1)S(1)}, u32[]{:S(2)}, u32[]{:S(2)}) %collective-permute-start.13) | collective-permute-done | bytes 200736 | tf_op jit(solution)/shard_map/ppermute | solution.py:320
  91.2 1.8 collective-permute-done.14.refs_8_
  93.0 1.9 collective-permute-start.6
  94.9 25.4 %shard_map.95 = (bf16[576,128]{1,0:T(8,128)(2,1)S(1)}, bf16[576,128]{1,0:T(8,128)(2,1)S(1)}, bf16[576,128]{1,0:T(8,128)(2,1)S(1)}, bf16[576,128]{1,0:T(8,128)(2,...) custom-call(s32[2]{0:T(128)S(1)} %copy-done.2, ...), custom_call_target="tpu_custom_call" | custom-call | flops 10000000000 | bytes 6000000 | tf_op jit(solution)/shard_map/pallas_call | solution.py:228
  120.4 13.1 %shard_map.96 = (bf16[288,128]{1,0:T(8,128)(2,1)S(1)}, bf16[288,128]{1,0:T(8,128)(2,1)S(1)}, bf16[288,128]{1,0:T(8,128)(2,1)S(1)}, bf16[288,128]{1,0:T(8,128)(2,...) custom-call(s32[2]{0:T(128)S(1)} %copy-done.2, ...), custom_call_target="tpu_custom_call", output_to_operand_aliasing={{8}: (11, {})} | custom-call | flops 10000000000 | bytes 6000000 | tf_op jit(solution)/shard_map/pallas_call | solution.py:228
  134.4 1.9 collective-permute-done.29
  137.3 5.6 %all-to-all-start.2 = ((bf16[16,48,384]{2,1,0:T(8,128)(2,1)}), bf16[16,48,384]{2,1,0:T(8,128)(2,1)S(1)}, u32[]{:S(2)}, u32[]{:S(2)}) async-start(bf16[16,48,384]{2,1,0:T(8,128)(2,1)} %add_convert_fusion), calls=%async_computation.2 | async-start | bytes 1179648 | tf_op jit(solution)/shard_map/all_to_all | solution.py:332
  143.4 1.7 collective-permute-start.16
  145.2 2.8 %collective-permute-start.25 = (bf16[576,128]{1,0:T(8,128)(2,1)S(1)}, bf16[576,128]{1,0:T(8,128)(2,1)S(1)}, u32[]{:S(2)}, u32[]{:S(2)}) collective-permute-start(bf16[576,128]{1,0:T(8,128)(2,1)S(1)} %get-tuple-element.77), channel_id=1, source_target_pairs={{0,4},{1,5},{2,6},{3,7},{4,0},{5,1},{6,2},{7,3},{8,12},{9,13},{10,... | collective-permute-start | bytes 442376 | tf_op jit(solution)/shard_map/ppermute | solution.py:320
  148.0 3.8 %collective-permute-done.16.refs_3_ = bf16[288,128]{1,0:T(8,128)(2,1)S(1)} collective-permute-done((bf16[288,128]{1,0:T(8,128)(2,1)S(1)}, bf16[288,128]{1,0:T(8,128)(2,1)S(1)}, u32[]{:S(2)}, u32[]{:S(2)}) %collective-permute-start.16) | collective-permute-done | bytes 73760 | tf_op jit(solution)/shard_map/ppermute | solution.py:320
  151.9 2.0 %collective-permute-start.27 = (bf16[576,128]{1,0:T(8,128)(2,1)S(1)}, bf16[576,128]{1,0:T(8,128)(2,1)S(1)}, u32[]{:S(2)}, u32[]{:S(2)}) collective-permute-start(bf16[576,128]{1,0:T(8,128)(2,1)S(1)} %get-tuple-element.79), channel_id=1, source_target_pairs={{0,6},{1,7},{2,4},{3,5},{4,2},{5,3},{6,0},{7,1},{8,14},{9,15},{10,... | collective-permute-start | bytes 442376 | tf_op jit(solution)/shard_map/ppermute | solution.py:320
  153.8 3.2 %collective-permute-start.28 = (bf16[576,128]{1,0:T(8,128)(2,1)S(1)}, bf16[576,128]{1,0:T(8,128)(2,1)S(1)}, u32[]{:S(2)}, u32[]{:S(2)}) collective-permute-start(bf16[576,128]{1,0:T(8,128)(2,1)S(1)} %get-tuple-element.80), channel_id=1, source_target_pairs={{0,7},{1,6},{2,5},{3,4},{4,3},{5,2},{6,1},{7,0},{8,15},{9,14},{10,... | collective-permute-start | bytes 442376 | tf_op jit(solution)/shard_map/ppermute | solution.py:320
  157.1 1.3 collective-permute-start.17
  158.8 10.9 %collective-permute-done.26.refs_6_ = bf16[576,128]{1,0:T(8,128)(2,1)S(1)} collective-permute-done((bf16[576,128]{1,0:T(8,128)(2,1)S(1)}, bf16[576,128]{1,0:T(8,128)(2,1)S(1)}, u32[]{:S(2)}, u32[]{:S(2)}) %collective-permute-start.26) | collective-permute-done | bytes 147488 | tf_op jit(solution)/shard_map/ppermute | solution.py:320
  169.7 3.1 %collective-permute-start.19 = (bf16[288,128]{1,0:T(8,128)(2,1)S(1)}, bf16[288,128]{1,0:T(8,128)(2,1)S(1)}, u32[]{:S(2)}, u32[]{:S(2)}) collective-permute-start(bf16[288,128]{1,0:T(8,128)(2,1)S(1)} %get-tuple-element.70), channel_id=1, source_target_pairs={{0,5},{1,4},{2,7},{3,6},{4,1},{5,0},{6,3},{7,2},{8,13},{9,12},{10,... | collective-permute-start | bytes 221192 | tf_op jit(solution)/shard_map/ppermute | solution.py:320
  172.8 4.5 %collective-permute-done.27.refs_7_ = bf16[576,128]{1,0:T(8,128)(2,1)S(1)} collective-permute-done((bf16[576,128]{1,0:T(8,128)(2,1)S(1)}, bf16[576,128]{1,0:T(8,128)(2,1)S(1)}, u32[]{:S(2)}, u32[]{:S(2)}) %collective-permute-start.27) | collective-permute-done | bytes 147488 | tf_op jit(solution)/shard_map/ppermute | solution.py:320
  177.3 6.2 %collective-permute-done.28.refs_8_ = bf16[576,128]{1,0:T(8,128)(2,1)S(1)} collective-permute-done((bf16[576,128]{1,0:T(8,128)(2,1)S(1)}, bf16[576,128]{1,0:T(8,128)(2,1)S(1)}, u32[]{:S(2)}, u32[]{:S(2)}) %collective-permute-start.28) | collective-permute-done | bytes 147488 | tf_op jit(solution)/shard_map/ppermute | solution.py:320
  184.4 4.0 %all-to-all-start.3 = ((bf16[8,24,96]{2,1,0:T(8,128)(2,1)}), bf16[8,24,96]{2,1,0:T(8,128)(2,1)S(1)}, u32[]{:S(2)}, u32[]{:S(2)}) async-start(bf16[8,24,96]{2,1,0:T(8,128)(2,1)} %bitcast.13), calls=%async_computation.3 | async-start | bytes 98304 | tf_op jit(solution)/shard_map/all_to_all | solution.py:332
  188.4 3.6 %shard_map.97 = (bf16[2,12,96,128]{3,2,1,0:T(8,128)(2,1)}, bf16[2,12,96,128]{3,2,1,0:T(8,128)(2,1)}, bf16[2,12,96,128]{3,2,1,0:T(8,128)(2,1)}) custom-call(s32[2]{0:T(128)} %pad_add_fusion.refs_0_.place, bf16[576,128]{1,0:T(8,128)(2,1)} %copy-done, bf16[576,128]{1,0:T(8,128)(2,1)} %copy-done.5, bf16[576,128]{1,0:T(8,128)(2,1)} %copy-done.6, ...), custom_call_target="tpu_custom_call" | custom-call | tf_op jit(solution)/shard_map/pallas_call | solution.py:281
  192.8 2.6 %shard_map.98 = (bf16[2,12,96,128]{3,2,1,0:T(8,128)(2,1)}, bf16[2,12,96,128]{3,2,1,0:T(8,128)(2,1)}, bf16[2,12,96,128]{3,2,1,0:T(8,128)(2,1)}) custom-call(s32[2]{0:T(128)} %pad_add_fusion.refs_0_.place, bf16[288,128]{1,0:T(8,128)(2,1)} %copy-done.1, bf16[288,128]{1,0:T(8,128)(2,1)} %copy-done.12, ...), custom_call_target="tpu_custom_call", output_to_operand_aliasing={{0}: (9, {}), {1}: (10, {}), {2}: (11, {})} | custom-call | tf_op jit(solution)/shard_map/pallas_call | solution.py:281
  (110 shorter events, 12.2 us)
Async XLA Ops:
  32.8 18.7 %collective-permute-start.7 = (bf16[16,48,384]{2,1,0:T(8,128)(2,1)S(1)}, bf16[16,48,384]{2,1,0:T(8,128)(2,1)S(1)}, u32[]{:S(2)}, u32[]{:S(2)}) collective-permute-start(bf16[16,48,384]{2,1,0:T(8,128)(2,1)S(1)} %all_to_all.21.own), channel_id=1, source_target_pairs={{0,1},{1,0},{2,3},{3,2},{4,5},{5,4},{6,7},{7,6},{8,9},{9,8},{10,11... | collective-permute-start | bytes 1769480 | tf_op jit(solution)/shard_map/ppermute | solution.py:320
  38.1 11.7 %collective-permute-start.8 = (bf16[784,128]{1,0:T(8,128)(2,1)}, bf16[784,128]{1,0:T(8,128)(2,1)S(1)}, u32[]{:S(2)}, u32[]{:S(2)}) collective-permute-start(bf16[784,128]{1,0:T(8,128)(2,1)} %get-tuple-element.56), channel_id=1, source_target_pairs={{0,1},{1,0},{2,3},{3,2},{4,5},{5,4},{6,7},{7,6},{8,9},{9,8},{10,11... | collective-permute-start | bytes 602120 | tf_op jit(solution)/shard_map/ppermute | solution.py:320
  38.7 12.0 %collective-permute-start.9 = (bf16[784,128]{1,0:T(8,128)(2,1)}, bf16[784,128]{1,0:T(8,128)(2,1)S(1)}, u32[]{:S(2)}, u32[]{:S(2)}) collective-permute-start(bf16[784,128]{1,0:T(8,128)(2,1)} %get-tuple-element.57), channel_id=1, source_target_pairs={{0,2},{1,3},{2,0},{3,1},{4,6},{5,7},{6,4},{7,5},{8,10},{9,11},{10,... | collective-permute-start | bytes 602120 | tf_op jit(solution)/shard_map/ppermute | solution.py:320
  43.4 1.5 collective-permute-start
  43.4 6.0 %collective-permute-start.1 = (bf16[384,128]{1,0:T(8,128)(2,1)}, bf16[384,128]{1,0:T(8,128)(2,1)S(1)}, u32[]{:S(2)}, u32[]{:S(2)}) collective-permute-start(bf16[384,128]{1,0:T(8,128)(2,1)} %get-tuple-element.49), channel_id=1, source_target_pairs={{0,2},{1,3},{2,0},{3,1},{4,6},{5,7},{6,4},{7,5},{8,10},{9,11},{10,... | collective-permute-start | bytes 294920 | tf_op jit(solution)/shard_map/ppermute | solution.py:320
  44.9 9.7 %collective-permute-start.10 = (bf16[784,128]{1,0:T(8,128)(2,1)S(1)}, bf16[784,128]{1,0:T(8,128)(2,1)S(1)}, u32[]{:S(2)}, u32[]{:S(2)}) collective-permute-start(bf16[784,128]{1,0:T(8,128)(2,1)S(1)} %copy-done.23), channel_id=1, source_target_pairs={{0,3},{1,2},{2,1},{3,0},{4,7},{5,6},{6,5},{7,4},{8,11},{9,10},{10,... | collective-permute-start | bytes 602120 | tf_op jit(solution)/shard_map/ppermute | solution.py:320
  49.3 22.4 %collective-permute-start.11 = (bf16[784,128]{1,0:T(8,128)(2,1)S(1)}, bf16[784,128]{1,0:T(8,128)(2,1)S(1)}, u32[]{:S(2)}, u32[]{:S(2)}) collective-permute-start(bf16[784,128]{1,0:T(8,128)(2,1)S(1)} %copy-done.22), channel_id=1, source_target_pairs={{0,4},{1,5},{2,6},{3,7},{4,0},{5,1},{6,2},{7,3},{8,12},{9,13},{10,... | collective-permute-start | bytes 602120 | tf_op jit(solution)/shard_map/ppermute | solution.py:320
  49.8 27.2 %collective-permute-start.12 = (bf16[784,128]{1,0:T(8,128)(2,1)S(1)}, bf16[784,128]{1,0:T(8,128)(2,1)S(1)}, u32[]{:S(2)}, u32[]{:S(2)}) collective-permute-start(bf16[784,128]{1,0:T(8,128)(2,1)S(1)} %copy-done.21), channel_id=1, source_target_pairs={{0,5},{1,4},{2,7},{3,6},{4,1},{5,0},{6,3},{7,2},{8,13},{9,12},{10,... | collective-permute-start | bytes 602120 | tf_op jit(solution)/shard_map/ppermute | solution.py:320
  50.6 40.2 %collective-permute-start.13 = (bf16[784,128]{1,0:T(8,128)(2,1)S(1)}, bf16[784,128]{1,0:T(8,128)(2,1)S(1)}, u32[]{:S(2)}, u32[]{:S(2)}) collective-permute-start(bf16[784,128]{1,0:T(8,128)(2,1)S(1)} %copy-done.20), channel_id=1, source_target_pairs={{0,6},{1,7},{2,4},{3,5},{4,2},{5,3},{6,0},{7,1},{8,14},{9,15},{10,... | collective-permute-start | bytes 602120 | tf_op jit(solution)/shard_map/ppermute | solution.py:320
  51.5 41.5 %collective-permute-start.14 = (bf16[784,128]{1,0:T(8,128)(2,1)S(1)}, bf16[784,128]{1,0:T(8,128)(2,1)S(1)}, u32[]{:S(2)}, u32[]{:S(2)}) collective-permute-start(bf16[784,128]{1,0:T(8,128)(2,1)S(1)} %copy-done.19), channel_id=1, source_target_pairs={{0,7},{1,6},{2,5},{3,4},{4,3},{5,2},{6,1},{7,0},{8,15},{9,14},{10,... | collective-permute-start | bytes 602120 | tf_op jit(solution)/shard_map/ppermute | solution.py:320
  54.6 65.7 %collective-permute-start.2 = (bf16[384,128]{1,0:T(8,128)(2,1)S(1)}, bf16[384,128]{1,0:T(8,128)(2,1)S(1)}, u32[]{:S(2)}, u32[]{:S(2)}) collective-permute-start(bf16[384,128]{1,0:T(8,128)(2,1)S(1)} %copy-done.28), channel_id=1, source_target_pairs={{0,3},{1,2},{2,1},{3,0},{4,7},{5,6},{6,5},{7,4},{8,11},{9,10},{10,... | collective-permute-start | bytes 294920 | tf_op jit(solution)/shard_map/ppermute | solution.py:320
  71.7 48.7 %collective-permute-start.3 = (bf16[384,128]{1,0:T(8,128)(2,1)S(1)}, bf16[384,128]{1,0:T(8,128)(2,1)S(1)}, u32[]{:S(2)}, u32[]{:S(2)}) collective-permute-start(bf16[384,128]{1,0:T(8,128)(2,1)S(1)} %copy-done.27), channel_id=1, source_target_pairs={{0,4},{1,5},{2,6},{3,7},{4,0},{5,1},{6,2},{7,3},{8,12},{9,13},{10,... | collective-permute-start | bytes 294920 | tf_op jit(solution)/shard_map/ppermute | solution.py:320
  77.1 43.3 %collective-permute-start.4 = (bf16[384,128]{1,0:T(8,128)(2,1)S(1)}, bf16[384,128]{1,0:T(8,128)(2,1)S(1)}, u32[]{:S(2)}, u32[]{:S(2)}) collective-permute-start(bf16[384,128]{1,0:T(8,128)(2,1)S(1)} %copy-done.26), channel_id=1, source_target_pairs={{0,5},{1,4},{2,7},{3,6},{4,1},{5,0},{6,3},{7,2},{8,13},{9,12},{10,... | collective-permute-start | bytes 294920 | tf_op jit(solution)/shard_map/ppermute | solution.py:320
  90.8 29.5 %collective-permute-start.5 = (bf16[384,128]{1,0:T(8,128)(2,1)S(1)}, bf16[384,128]{1,0:T(8,128)(2,1)S(1)}, u32[]{:S(2)}, u32[]{:S(2)}) collective-permute-start(bf16[384,128]{1,0:T(8,128)(2,1)S(1)} %copy-done.25), channel_id=1, source_target_pairs={{0,6},{1,7},{2,4},{3,5},{4,2},{5,3},{6,0},{7,1},{8,14},{9,15},{10,... | collective-permute-start | bytes 294920 | tf_op jit(solution)/shard_map/ppermute | solution.py:320
  93.0 27.4 %collective-permute-start.6 = (bf16[384,128]{1,0:T(8,128)(2,1)S(1)}, bf16[384,128]{1,0:T(8,128)(2,1)S(1)}, u32[]{:S(2)}, u32[]{:S(2)}) collective-permute-start(bf16[384,128]{1,0:T(8,128)(2,1)S(1)} %copy-done.24), channel_id=1, source_target_pairs={{0,7},{1,6},{2,5},{3,4},{4,3},{5,2},{6,1},{7,0},{8,15},{9,14},{10,... | collective-permute-start | bytes 294920 | tf_op jit(solution)/shard_map/ppermute | solution.py:320
  134.3 2.1 %collective-permute-start.29 = (bf16[16,48,384]{2,1,0:T(8,128)(2,1)S(1)}, bf16[16,48,384]{2,1,0:T(8,128)(2,1)S(1)}, u32[]{:S(2)}, u32[]{:S(2)}) collective-permute-start(bf16[16,48,384]{2,1,0:T(8,128)(2,1)S(1)} %get-tuple-element.89), channel_id=1, source_target_pairs={{0,1},{1,0},{2,3},{3,2},{4,5},{5,4},{6,7},{7,6},{8,9},{9,8},{10,11... | collective-permute-start | bytes 1769480 | tf_op jit(solution)/shard_map/ppermute | solution.py:320
  137.3 46.2 %all-to-all-start.2 = ((bf16[16,48,384]{2,1,0:T(8,128)(2,1)}), bf16[16,48,384]{2,1,0:T(8,128)(2,1)S(1)}, u32[]{:S(2)}, u32[]{:S(2)}) async-start(bf16[16,48,384]{2,1,0:T(8,128)(2,1)} %add_convert_fusion), calls=%async_computation.2 | async-start | bytes 1179648 | tf_op jit(solution)/shard_map/all_to_all | solution.py:332
  142.9 8.9 %collective-permute-start.22 = (bf16[576,128]{1,0:T(8,128)(2,1)S(1)}, bf16[576,128]{1,0:T(8,128)(2,1)S(1)}, u32[]{:S(2)}, u32[]{:S(2)}) collective-permute-start(bf16[576,128]{1,0:T(8,128)(2,1)S(1)} %get-tuple-element.74), channel_id=1, source_target_pairs={{0,1},{1,0},{2,3},{3,2},{4,5},{5,4},{6,7},{7,6},{8,9},{9,8},{10,11... | collective-permute-start | bytes 442376 | tf_op jit(solution)/shard_map/ppermute | solution.py:320
  142.9 10.9 %collective-permute-start.23 = (bf16[576,128]{1,0:T(8,128)(2,1)S(1)}, bf16[576,128]{1,0:T(8,128)(2,1)S(1)}, u32[]{:S(2)}, u32[]{:S(2)}) collective-permute-start(bf16[576,128]{1,0:T(8,128)(2,1)S(1)} %get-tuple-element.75), channel_id=1, source_target_pairs={{0,2},{1,3},{2,0},{3,1},{4,6},{5,7},{6,4},{7,5},{8,10},{9,11},{10,... | collective-permute-start | bytes 442376 | tf_op jit(solution)/shard_map/ppermute | solution.py:320
  143.0 2.2 %collective-permute-start.15 = (bf16[288,128]{1,0:T(8,128)(2,1)S(1)}, bf16[288,128]{1,0:T(8,128)(2,1)S(1)}, u32[]{:S(2)}, u32[]{:S(2)}) collective-permute-start(bf16[288,128]{1,0:T(8,128)(2,1)S(1)} %get-tuple-element.66), channel_id=1, source_target_pairs={{0,1},{1,0},{2,3},{3,2},{4,5},{5,4},{6,7},{7,6},{8,9},{9,8},{10,11... | collective-permute-start | bytes 221192 | tf_op jit(solution)/shard_map/ppermute | solution.py:320
  143.4 8.4 %collective-permute-start.16 = (bf16[288,128]{1,0:T(8,128)(2,1)S(1)}, bf16[288,128]{1,0:T(8,128)(2,1)S(1)}, u32[]{:S(2)}, u32[]{:S(2)}) collective-permute-start(bf16[288,128]{1,0:T(8,128)(2,1)S(1)} %get-tuple-element.67), channel_id=1, source_target_pairs={{0,2},{1,3},{2,0},{3,1},{4,6},{5,7},{6,4},{7,5},{8,10},{9,11},{10,... | collective-permute-start | bytes 221192 | tf_op jit(solution)/shard_map/ppermute | solution.py:320
  145.2 11.9 %collective-permute-start.24 = (bf16[576,128]{1,0:T(8,128)(2,1)S(1)}, bf16[576,128]{1,0:T(8,128)(2,1)S(1)}, u32[]{:S(2)}, u32[]{:S(2)}) collective-permute-start(bf16[576,128]{1,0:T(8,128)(2,1)S(1)} %get-tuple-element.76), channel_id=1, source_target_pairs={{0,3},{1,2},{2,1},{3,0},{4,7},{5,6},{6,5},{7,4},{8,11},{9,10},{10,... | collective-permute-start | bytes 442376 | tf_op jit(solution)/shard_map/ppermute | solution.py:320
  145.2 13.7 %collective-permute-start.25 = (bf16[576,128]{1,0:T(8,128)(2,1)S(1)}, bf16[576,128]{1,0:T(8,128)(2,1)S(1)}, u32[]{:S(2)}, u32[]{:S(2)}) collective-permute-start(bf16[576,128]{1,0:T(8,128)(2,1)S(1)} %get-tuple-element.77), channel_id=1, source_target_pairs={{0,4},{1,5},{2,6},{3,7},{4,0},{5,1},{6,2},{7,3},{8,12},{9,13},{10,... | collective-permute-start | bytes 442376 | tf_op jit(solution)/shard_map/ppermute | solution.py:320
  151.8 17.9 %collective-permute-start.26 = (bf16[576,128]{1,0:T(8,128)(2,1)S(1)}, bf16[576,128]{1,0:T(8,128)(2,1)S(1)}, u32[]{:S(2)}, u32[]{:S(2)}) collective-permute-start(bf16[576,128]{1,0:T(8,128)(2,1)S(1)} %get-tuple-element.78), channel_id=1, source_target_pairs={{0,5},{1,4},{2,7},{3,6},{4,1},{5,0},{6,3},{7,2},{8,13},{9,12},{10,... | collective-permute-start | bytes 442376 | tf_op jit(solution)/shard_map/ppermute | solution.py:320
  151.9 25.5 %collective-permute-start.27 = (bf16[576,128]{1,0:T(8,128)(2,1)S(1)}, bf16[576,128]{1,0:T(8,128)(2,1)S(1)}, u32[]{:S(2)}, u32[]{:S(2)}) collective-permute-start(bf16[576,128]{1,0:T(8,128)(2,1)S(1)} %get-tuple-element.79), channel_id=1, source_target_pairs={{0,6},{1,7},{2,4},{3,5},{4,2},{5,3},{6,0},{7,1},{8,14},{9,15},{10,... | collective-permute-start | bytes 442376 | tf_op jit(solution)/shard_map/ppermute | solution.py:320
  153.8 29.7 %collective-permute-start.28 = (bf16[576,128]{1,0:T(8,128)(2,1)S(1)}, bf16[576,128]{1,0:T(8,128)(2,1)S(1)}, u32[]{:S(2)}, u32[]{:S(2)}) collective-permute-start(bf16[576,128]{1,0:T(8,128)(2,1)S(1)} %get-tuple-element.80), channel_id=1, source_target_pairs={{0,7},{1,6},{2,5},{3,4},{4,3},{5,2},{6,1},{7,0},{8,15},{9,14},{10,... | collective-permute-start | bytes 442376 | tf_op jit(solution)/shard_map/ppermute | solution.py:320
  157.1 35.0 %collective-permute-start.17 = (bf16[288,128]{1,0:T(8,128)(2,1)S(1)}, bf16[288,128]{1,0:T(8,128)(2,1)S(1)}, u32[]{:S(2)}, u32[]{:S(2)}) collective-permute-start(bf16[288,128]{1,0:T(8,128)(2,1)S(1)} %get-tuple-element.68), channel_id=1, source_target_pairs={{0,3},{1,2},{2,1},{3,0},{4,7},{5,6},{6,5},{7,4},{8,11},{9,10},{10,... | collective-permute-start | bytes 221192 | tf_op jit(solution)/shard_map/ppermute | solution.py:320
  158.8 33.2 %collective-permute-start.18 = (bf16[288,128]{1,0:T(8,128)(2,1)S(1)}, bf16[288,128]{1,0:T(8,128)(2,1)S(1)}, u32[]{:S(2)}, u32[]{:S(2)}) collective-permute-start(bf16[288,128]{1,0:T(8,128)(2,1)S(1)} %get-tuple-element.69), channel_id=1, source_target_pairs={{0,4},{1,5},{2,6},{3,7},{4,0},{5,1},{6,2},{7,3},{8,12},{9,13},{10,... | collective-permute-start | bytes 221192 | tf_op jit(solution)/shard_map/ppermute | solution.py:320
  169.7 22.4 %collective-permute-start.19 = (bf16[288,128]{1,0:T(8,128)(2,1)S(1)}, bf16[288,128]{1,0:T(8,128)(2,1)S(1)}, u32[]{:S(2)}, u32[]{:S(2)}) collective-permute-start(bf16[288,128]{1,0:T(8,128)(2,1)S(1)} %get-tuple-element.70), channel_id=1, source_target_pairs={{0,5},{1,4},{2,7},{3,6},{4,1},{5,0},{6,3},{7,2},{8,13},{9,12},{10,... | collective-permute-start | bytes 221192 | tf_op jit(solution)/shard_map/ppermute | solution.py:320
  177.3 14.8 %collective-permute-start.20 = (bf16[288,128]{1,0:T(8,128)(2,1)S(1)}, bf16[288,128]{1,0:T(8,128)(2,1)S(1)}, u32[]{:S(2)}, u32[]{:S(2)}) collective-permute-start(bf16[288,128]{1,0:T(8,128)(2,1)S(1)} %get-tuple-element.71), channel_id=1, source_target_pairs={{0,6},{1,7},{2,4},{3,5},{4,2},{5,3},{6,0},{7,1},{8,14},{9,15},{10,... | collective-permute-start | bytes 221192 | tf_op jit(solution)/shard_map/ppermute | solution.py:320
  183.5 8.6 %collective-permute-start.21 = (bf16[288,128]{1,0:T(8,128)(2,1)S(1)}, bf16[288,128]{1,0:T(8,128)(2,1)S(1)}, u32[]{:S(2)}, u32[]{:S(2)}) collective-permute-start(bf16[288,128]{1,0:T(8,128)(2,1)S(1)} %get-tuple-element.72), channel_id=1, source_target_pairs={{0,7},{1,6},{2,5},{3,4},{4,3},{5,2},{6,1},{7,0},{8,15},{9,14},{10,... | collective-permute-start | bytes 221192 | tf_op jit(solution)/shard_map/ppermute | solution.py:320
  184.4 11.1 %all-to-all-start.3 = ((bf16[8,24,96]{2,1,0:T(8,128)(2,1)}), bf16[8,24,96]{2,1,0:T(8,128)(2,1)S(1)}, u32[]{:S(2)}, u32[]{:S(2)}) async-start(bf16[8,24,96]{2,1,0:T(8,128)(2,1)} %bitcast.13), calls=%async_computation.3 | async-start | bytes 98304 | tf_op jit(solution)/shard_map/all_to_all | solution.py:332
  (29 other events, 537.9 us)
where the time goes:
time: 198 us; the launch traced here: 196 us
  waiting for transfers between devices  62.4 us (32%)
  Pallas kernels  54.1 us (27%)
  starting transfers between devices  42.7 us (22%)
  blocking collectives  31.1 us (16%)
  other arithmetic  3.15 us (2%)
    ppermute x30, waiting for transfers between devices, swapped(): return lax.ppermute(value, axes, [(i, i ^ k) for i in range(count)])  62.4 us
    pallas_call x2, Pallas kernels, attention(): pl.pallas_call(lambda *refs: attention_body(*refs, first_row=first_row, r...  38.5 us
    ppermute x30, starting transfers between devices, swapped(): return lax.ppermute(value, axes, [(i, i ^ k) for i in range(count)])  33.1 us
    all_to_all x2, blocking collectives, exchanged(): return lax.all_to_all(value, axes, split_axis=0, concat_axis=0, tiled=True)  31.1 us
    all_to_all x2, starting transfers between devices, exchanged(): return lax.all_to_all(value, axes, split_axis=0, concat_axis=0, tiled=True)  9.55 us
    pallas_call x2, Pallas kernels, pack(): pl.pallas_call(lambda *refs: pack_body(*refs, with_mask=mask is not None)...  7.88 us
    pallas_call x2, Pallas kernels, unpack(): pl.pallas_call(lambda *refs: unpack_body(*refs), grid=(1,), in_specs=[sma...  6.27 us
  transfers between devices with their start and end apart: 32, of which 12 were waited for; matrix products, arithmetic and copies ran while one was open for 1% of the time, Pallas kernels for 21%

commit v1 on v0

--- a/solution.py
+++ b/solution.py
@@ -16,20 +16,25 @@
 COL = ("z", "core")
 PLANE = ("x", "y")
 COLUMN = ("zh", "z")
-CHUNKS = ((0, 8), (8, 4))
+CHUNKS = ((0, 4), (4, 4), (8, 4))
+SENDS = ((0, 8), (8, 4))
 GROUP = 4
+STRIP = 768
 FAR_FIRST = (6, 7, 4, 5, 2, 3, 1)
 TILE = 256
 BF16 = jnp.bfloat16
 F32 = jnp.float32
 
+LOG2E = math.log2(math.e)
+
 
 def lane_slot(shape):
     return lax.broadcasted_iota(jnp.int32, shape, len(shape) - 1) // HEAD_DIM
 
 
 def turned(value, slots):
-    return pltpu.roll(value, (slots * HEAD_DIM) & (LANES - 1), value.ndim - 1)
+    shift = slots * HEAD_DIM & (LANES - 1)
+    return value if isinstance(shift, int) and shift == 0 else pltpu.roll(value, shift, value.ndim - 1)
 
 
 def small_input():
@@ -43,7 +48,7 @@
 def pack_body(place, *refs, with_mask):
     tensors = refs[:4]
     mask = refs[4] if with_mask else None
-    outs = refs[-8:]
+    outs, held = refs[-9:-1], refs[-1]
     z, core = place[0], place[1]
     rows, queries = tensors[0].shape[1], tensors[0].shape[2]
     slot = lane_slot((queries, LANES))
@@ -51,14 +56,15 @@
     def one_row(r, carry):
         for kc in range(2):
             half = core ^ kc
-            parts = [t[half, r].astype(F32) for t in tensors]
+            parts = [t[half, r] for t in tensors]
+            for head in range(HEADS):
+                packed = turned(parts[0], -head)
+                for t in range(1, 4):
+                    packed = jnp.where(slot == t, turned(parts[t], t - head), packed)
+                held[head] = packed
+            start = pl.multiple_of(r * queries, 16)
             for kz in range(4):
-                head = z ^ kz
-                packed = turned(parts[0], 4 - head)
-                for t in range(1, 4):
-                    packed = jnp.where(slot == t, turned(parts[t], 4 + t - head), packed)
-                start = pl.multiple_of(r * queries, 16)
-                outs[kz * 2 + kc][pl.ds(start, queries), :] = packed.astype(BF16)
+                outs[kz * 2 + kc][pl.ds(start, queries), :] = held[z ^ kz]
         return carry
 
     lax.fori_loop(0, rows, one_row, 0)
@@ -88,6 +94,7 @@
         in_specs=[small_input()] + specs,
         out_specs=[pl.BlockSpec((length, LANES), lambda i: (0, 0))] * 8,
         out_shape=[jax.ShapeDtypeStruct((length, LANES), BF16)] * 8,
+        scratch_shapes=[pltpu.VMEM((HEADS, queries, LANES), BF16)],
         cost_estimate=pl.CostEstimate(flops=10**9, bytes_accessed=2 * 10**6, transcendentals=0),
     )(place, *operands)
 
@@ -96,20 +103,23 @@
     return (k & 1) * 4 + (place[0] ^ (k >> 1))
 
 
-def attention_body(place, *refs, first_row, rows):
-    first = first_row == 0
-    tiles = refs[:8]
-    bias = refs[8]
+def attention_body(place, *refs, first, first_row, rows, held_count):
+    tiles, refs = refs[:8], refs[8:]
+    held, refs = refs[:held_count], refs[held_count:]
+    bias, refs = refs[0], refs[1:]
+    if not first:
+        mask_lanes, bias_grad_in, refs = refs[0], refs[1], refs[2:]
+    outs, bias_grad, refs = refs[:8], refs[8], refs[9:]
     if first:
-        (outs, bias_grad, mask_out), scratch = (refs[9:17], refs[17], refs[18]), refs[19:]
-        mask_lanes = mask_out
-    else:
-        mask_lanes, bias_grad_in = refs[9], refs[10]
-        (outs, bias_grad), scratch = (refs[11:19], refs[19]), refs[20:]
-    pairs, probs, scores_low, logits, grad_probs, key_sum, value_sum, query_sum, masked = scratch
+        mask_lanes, refs = refs[0], refs[1:]
+        mask_out = mask_lanes
+    scratch = refs
+    held_groups = 0 if not held else held[0].shape[0] // (3 * (bias.shape[0] // 8))
+    pairs, left_key, left_value, masked, probs, scores_low, l0, l1, l2, g0, g1, g2, key_sum, value_sum, query_sum = scratch
+    logits_all, grad_probs_all = (l0, l1, l2), (g0, g1, g2)
+    zero_row = place[2]
     length = pairs.shape[0]
     block = length // 8
-    strip = block
     scale = 1.0 / math.sqrt(HEAD_DIM)
 
     if first:
@@ -132,66 +142,71 @@
 
     def one_row(r, carry):
         for k in range(8):
+            source = pl.ds(pl.multiple_of(r * block, 16), block)
             start = pl.multiple_of(position(place, k) * block, 16)
-            source = pl.multiple_of(r * block, 16)
-            pairs[pl.ds(start, block), :] = tiles[k][pl.ds(source, block), :]
-        slot = lane_slot((length, LANES))
-        wide = pairs[...].astype(F32)
-        zero = jnp.zeros_like(wide)
-        query_at_key = jnp.where(slot == 1, pltpu.roll(wide, HEAD_DIM, 1), zero).astype(BF16)
-        grad_at_value = jnp.where(slot == 2, pltpu.roll(wide, LANES - HEAD_DIM, 1), zero).astype(BF16)
+            pairs[pl.ds(start, block), :] = tiles[k][source, :]
         group, in_group = r // GROUP, r % GROUP
-        query_at_row = jnp.where(slot == in_group, turned(wide, in_group), zero).astype(BF16)
-        grad_at_row = jnp.where(slot == in_group, turned(wide, in_group + 1), zero).astype(BF16)
-        keys_turned = jnp.transpose(wide)[HEAD_DIM : 2 * HEAD_DIM, :].astype(BF16)
+        slot = lane_slot((block, LANES))
         chosen = (lax.broadcasted_iota(jnp.int32, (LANES, LANES), 0) == r + first_row).astype(BF16)
-        masked[...] = 1000000000.0 * (
-            jnp.dot(mask_lanes[...], chosen, preferred_element_type=F32) - 1.0
-        )
-        for j in range(0, length, TILE):
-            right_query = query_at_key[j : j + TILE]
-            right_grad = grad_at_value[j : j + TILE]
+        for i in range(0, length, block):
+            own = slice(i, i + block)
+            wide = pltpu.roll(pairs[own, :].astype(F32), LANES - HEAD_DIM, 1)
+            left_key[own, :] = jnp.where(slot == 0, wide, 0.0).astype(BF16)
+            wide = pltpu.roll(wide, 2 * HEAD_DIM, 1)
+            left_value[own, :] = jnp.where(slot == 3, wide, 0.0).astype(BF16)
+            present = jnp.dot(mask_lanes[own, :], chosen, preferred_element_type=F32)
+            masked[own, :] = (1000000000.0 * LOG2E) * (present - 1.0)
+        keys_turned = jnp.transpose(pairs[...].astype(F32))[HEAD_DIM : 2 * HEAD_DIM, :].astype(BF16)
+        for tile, j in enumerate(range(0, length, TILE)):
+            logits, grad_probs = logits_all[tile], grad_probs_all[tile]
+            right = pairs[j : j + TILE, :]
             top = jnp.full((8, TILE), -jnp.inf, F32)
-            for i in range(0, length, strip):
-                s = lax.dot_general(
-                    pairs[i : i + strip, :],
-                    right_query,
+            for i in range(0, length, STRIP):
+                t = lax.dot_general(
+                    left_key[i : i + STRIP, :],
+                    right,
                     (((1,), (1,)), ((), ())),
                     preferred_element_type=F32,
                 )
-                mask_strip = masked[i : i + strip, :]
+                mask_strip = masked[i : i + STRIP, :]
                 t = (
-                    s * scale
-                    + bias[i : i + strip, j : j + TILE]
+                    t * (scale * LOG2E)
+                    + bias[i : i + STRIP, j : j + TILE]
                     + jnp.concatenate([mask_strip] * (TILE // LANES), axis=1)
                 )
-                logits[i : i + strip, :] = t
-                top = jnp.maximum(top, jnp.max(t.reshape(strip // 8, 8, TILE), axis=0))
+                logits[i : i + STRIP, :] = t
+                top = jnp.maximum(top, jnp.max(t.reshape(STRIP // 8, 8, TILE), axis=0))
+            for i in range(0, length, STRIP):
+                grad_probs[i : i + STRIP, :] = lax.dot_general(
+                    left_value[i : i + STRIP, :],
+                    right,
+                    (((1,), (1,)), ((), ())),
+                    preferred_element_type=F32,
+                )
             top = jnp.max(top, axis=0, keepdims=True)
             total = jnp.zeros((8, TILE), F32)
             delta = jnp.zeros((8, TILE), F32)
-            for i in range(0, length, strip):
-                gp = lax.dot_general(
-                    pairs[i : i + strip, :],
-                    right_grad,
-                    (((1,), (1,)), ((), ())),
-                    preferred_element_type=F32,
-                )
-                e = jnp.exp(logits[i : i + strip, :] - top)
-                logits[i : i + strip, :] = e
-                grad_probs[i : i + strip, :] = gp
-                total = total + jnp.sum(e.reshape(strip // 8, 8, TILE), axis=0)
-                delta = delta + jnp.sum((e * gp).reshape(strip // 8, 8, TILE), axis=0)
+            for i in range(0, length, 32):
+                held = pl.ds(pl.multiple_of(zero_row + i, 8), 32)
+                gp = grad_probs[i : i + 32, :]
+                e = jnp.exp2(logits[i : i + 32, :] - top)
+                logits[i : i + 32, :] = e
+                total = total + jnp.sum(e.reshape(4, 8, TILE), axis=0)
+                delta = delta + jnp.sum((e * gp).reshape(4, 8, TILE), axis=0)
             inverse = 1.0 / jnp.sum(total, axis=0, keepdims=True)
             delta = jnp.sum(delta, axis=0, keepdims=True) * inverse
-            for i in range(0, length, strip):
-                p = logits[i : i + strip, :] * inverse
-                ds = p * (grad_probs[i : i + strip, :] - delta)
-                probs[i : i + strip, j : j + TILE] = p.astype(BF16)
-                scores_low[i : i + strip, j : j + TILE] = ds.astype(BF16)
-                bias_grad[i : i + strip, j : j + TILE] += ds
-        value_sum[group] += jnp.dot(probs[...], grad_at_row, preferred_element_type=F32)
-        key_sum[group] += jnp.dot(scores_low[...], query_at_row, preferred_element_type=F32)
+            for i in range(0, length, 32):
+                held = pl.ds(pl.multiple_of(zero_row + i, 8), 32)
+                p = logits[held, :] * inverse
+                ds = p * (grad_probs[held, :] - delta)
+                probs[i : i + 32, j : j + TILE] = p.astype(BF16)
+                scores_low[i : i + 32, j : j + TILE] = ds.astype(BF16)
+                bias_grad[i : i + 32, j : j + TILE] += ds
+        slot = lane_slot((length, LANES))
+        value_row = jnp.dot(probs[...], pairs[...], preferred_element_type=F32)
+        value_sum[group] = jnp.where(slot == in_group, turned(value_row, in_group + 1), value_sum[group])
+        key_row = jnp.dot(scores_low[...], pairs[...], preferred_element_type=F32)
+        key_sum[group] = jnp.where(slot == in_group, turned(key_row, in_group), key_sum[group])
         query_sum[pl.ds(pl.multiple_of(r * HEAD_DIM, 32), HEAD_DIM), :] = jnp.dot(
             keys_turned, scores_low[...], preferred_element_type=F32
         )
@@ -205,47 +220,55 @@
         scores_low[:, pl.ds((groups + g) * LANES, LANES)] = value_sum[g].astype(BF16)
     for k in range(8):
         start = pl.multiple_of(position(place, k) * block, 16)
-        for g in range(3 * groups):
-            held, lane = (probs, g) if g < groups else (scores_low, g - groups)
-            outs[k][g * block : (g + 1) * block, :] = held[
-                pl.ds(start, block), lane * LANES : (lane + 1) * LANES
-            ]
-
-
-def attention(place, tiles, bias, mask_lanes, bias_grad, chunk):
+        for t in range(3):
+            for g in range(held_groups + groups):
+                line = (t * (held_groups + groups) + g) * block
+                if g < held_groups:
+                    own = (t * held_groups + g) * block
+                    outs[k][line : line + block, :] = held[k][own : own + block, :]
+                    continue
+                source, lane = (probs, 0) if t == 0 else (scores_low, (t - 1) * groups)
+                lane = (lane + g - held_groups) * LANES
+                outs[k][line : line + block, :] = source[pl.ds(start, block), lane : lane + LANES]
+
+
+def attention(place, tiles, held, bias, mask_lanes, bias_grad, chunk):
     first = chunk == 0
     first_row, rows = CHUNKS[chunk]
     groups = rows // GROUP
     length = bias.shape[0]
     block = length // 8
-    operands = [*tiles, bias]
+    place = jnp.concatenate([place, jnp.zeros((1,), jnp.int32)])
+    operands = [*tiles, *held, bias]
     if not first:
         operands += [mask_lanes, bias_grad]
-    out_shape = [jax.ShapeDtypeStruct((3 * groups * block, LANES), BF16)] * 8
+    lines = 3 * groups * block + (held[0].shape[0] if held else 0)
+    out_shape = [jax.ShapeDtypeStruct((lines, LANES), BF16)] * 8
     out_shape.append(jax.ShapeDtypeStruct((length, length), F32))
     if first:
         out_shape.append(jax.ShapeDtypeStruct((length, LANES), BF16))
     results = pl.pallas_call(
-        lambda *refs: attention_body(*refs, first_row=first_row, rows=rows),
+        lambda *refs: attention_body(
+            *refs, first=first, first_row=first_row, rows=rows, held_count=len(held)
+        ),
         in_specs=[small_input()] + in_vmem(len(operands)),
         out_specs=in_vmem(len(out_shape)),
         out_shape=out_shape,
         scratch_shapes=[
-            pltpu.VMEM((length, LANES), BF16),
+            *[pltpu.VMEM((length, LANES), BF16)] * 3,
+            pltpu.VMEM((length, LANES), F32),
             pltpu.VMEM((length, length), BF16),
             pltpu.VMEM((length, length), BF16),
-            pltpu.VMEM((length, TILE), F32),
-            pltpu.VMEM((length, TILE), F32),
+            *[pltpu.VMEM((length, TILE), F32)] * 6,
             pltpu.VMEM((groups, length, LANES), F32),
             pltpu.VMEM((groups, length, LANES), F32),
             pltpu.VMEM((groups * LANES, length), F32),
-            pltpu.VMEM((length, LANES), F32),
         ],
         input_output_aliases={} if first else {len(operands): 8},
         cost_estimate=pl.CostEstimate(
             flops=10**10, bytes_accessed=6 * 10**6, transcendentals=length * length * rows
         ),
-        compiler_params=pltpu.CompilerParams(vmem_limit_bytes=40 * 2**20),
+        compiler_params=pltpu.CompilerParams(vmem_limit_bytes=18 * 2**20),
     )(place, *operands)
     if first:
         return results[:8], results[8], results[9]
@@ -254,7 +277,7 @@
 
 def unpack_body(place, *refs):
     parts = refs[:8]
-    outs = refs[-3:]
+    outs, held = refs[-4:-1], refs[-1]
     z, core = place[0], place[1]
     rows, queries = outs[0].shape[1], outs[0].shape[2]
     groups = rows // GROUP
@@ -262,19 +285,20 @@
     for kc in range(2):
         half = core ^ kc
         for g in range(3 * groups):
-            heads = [parts[kz * 2 + kc][g * queries : (g + 1) * queries, :].astype(F32) for kz in range(4)]
+            for kz in range(4):
+                held[z ^ kz] = parts[kz * 2 + kc][g * queries : (g + 1) * queries, :]
+            heads = [held[h] for h in range(HEADS)]
             for r in range(GROUP):
-                row = turned(heads[0], 4 + z - r)
-                for kz in range(1, 4):
-                    head = z ^ kz
-                    row = jnp.where(slot == head, turned(heads[kz], 4 + head - r), row)
-                outs[g // groups][half, g % groups * GROUP + r] = row.astype(BF16)
+                row = turned(heads[0], -r)
+                for h in range(1, HEADS):
+                    row = jnp.where(slot == h, turned(heads[h], h - r), row)
+                outs[g // groups][half, g % groups * GROUP + r] = row
 
 
 def unpack(place, parts, outs, chunk, shape):
     first = outs is None
     halves, _, queries, lanes = shape
-    first_row, rows = CHUNKS[chunk]
+    first_row, rows = SENDS[chunk]
     block = pl.BlockSpec((halves, rows, queries, lanes), lambda i: (0, first_row // rows, 0, 0))
     piece = pl.BlockSpec(parts[0].shape, lambda i: (0, 0))
     kept = [] if first else list(outs)
@@ -284,6 +308,7 @@
         in_specs=[small_input()] + [piece] * 8 + [pl.BlockSpec(memory_space=pl.ANY)] * len(kept),
         out_specs=[block] * 3,
         out_shape=[jax.ShapeDtypeStruct(shape, BF16)] * 3,
+        scratch_shapes=[pltpu.VMEM((HEADS, queries, lanes), BF16)],
         input_output_aliases={} if first else {9: 0, 10: 1, 11: 2},
     )(place, *parts, *kept)
 
@@ -303,8 +328,8 @@
     length = out.shape[0]
     half = length // 2
     for row, line, part, start in bias_rows(place, length):
-        out[pl.ds(start, part), :half] = own[row, line : line + part, :].astype(F32)
-        out[pl.ds(start, part), half:] = other[row, line : line + part, :].astype(F32)
+        out[pl.ds(start, part), :half] = own[row, line : line + part, :].astype(F32) * LOG2E
+        out[pl.ds(start, part), half:] = other[row, line : line + part, :].astype(F32) * LOG2E
 
 
 def bias_out_body(place, whole, own, other):
@@ -379,18 +404,18 @@
     place = jnp.stack([lax.axis_index("z"), lax.axis_index("core")]).astype(jnp.int32)
     tensors = [t.reshape(shape) for t in (query_proj, key_proj, value_proj, grad_out)]
     bias = gathered_bias(place, pair_bias)
-    chunks = range(len(CHUNKS))
     arrived = []
-    for chunk in chunks:
+    for chunk in range(len(CHUNKS)):
         packed = pack(place, tensors, pair_mask if chunk == 0 else None, chunk)
         arrived.append(sent(packed))
-    outs = mask_lanes = bias_grad = None
-    returned = []
-    for chunk in chunks:
-        grads, bias_grad, mask_lanes = attention(place, arrived[chunk], bias, mask_lanes, bias_grad, chunk)
-        returned.append(sent(grads))
+    grads, bias_grad, mask_lanes = attention(place, arrived[0], [], bias, None, None, 0)
+    grads, bias_grad, mask_lanes = attention(place, arrived[1], grads, bias, mask_lanes, bias_grad, 1)
+    returned = [sent(grads)]
+    grads, bias_grad, mask_lanes = attention(place, arrived[2], [], bias, mask_lanes, bias_grad, 2)
+    returned.append(sent(grads))
     grad_bias = reduced_bias(place, bias_grad, HEADS)
-    for chunk in chunks:
+    outs = None
+    for chunk in range(len(SENDS)):
         outs = unpack(place, returned[chunk], outs, chunk, shape)
     grads = [o.reshape(query_proj.shape) for o in outs]
     return (*grads, grad_bias)

time: 198 us -> 182 us (0.919)
  waiting for transfers between devices: 62.4 us -> 40 us
  starting transfers between devices: 42.7 us -> 54.3 us
  Pallas kernels: 54.1 us -> 48.1 us
    ppermute x30 -> x37, waiting for transfers between devices: 62.4 us -> 39.6 us  [swapped(): return lax.ppermute(value, axes, [(i, i ^ k) for i in range(count)])]
    pallas_call x2 -> x3, Pallas kernels: 38.5 us -> 31.6 us  [attention(): pl.pallas_call(lambda *refs: attention_body(*refs, first=first, first_row...]
    ppermute x30 -> x37, starting transfers between devices: 33.1 us -> 39.5 us  [swapped(): return lax.ppermute(value, axes, [(i, i ^ k) for i in range(count)])]
    all_to_all x2, starting transfers between devices: 9.55 us -> 14.9 us  [exchanged(): return lax.all_to_all(value, axes, split_axis=0, concat_axis=0, tiled=True)]
    pallas_call x2 -> x3, Pallas kernels: 7.88 us -> 9.16 us  [pack(): pl.pallas_call(lambda *refs: pack_body(*refs, with_mask=mask is not None)...]
  transfers between devices with their start and end apart: 32 -> 39, of which waited for: 12 -> 12; matrix products, arithmetic and copies ran while one was open for 1% -> 1% of each run, Pallas kernels for 21% -> 21%
where the time goes in v1:
time: 182 us; the launch traced here: 180 us
  starting transfers between devices  54.3 us (30%)
  Pallas kernels  48.1 us (26%)
  waiting for transfers between devices  40 us (22%)
  blocking collectives  31.1 us (17%)
  other arithmetic  3.24 us (2%)
    ppermute x37, waiting for transfers between devices, swapped(): return lax.ppermute(value, axes, [(i, i ^ k) for i in range(count)])  39.6 us
    ppermute x37, starting transfers between devices, swapped(): return lax.ppermute(value, axes, [(i, i ^ k) for i in range(count)])  39.5 us
    pallas_call x3, Pallas kernels, attention(): pl.pallas_call(lambda *refs: attention_body(*refs, first=first, first_row...  31.6 us
    all_to_all x2, blocking collectives, exchanged(): return lax.all_to_all(value, axes, split_axis=0, concat_axis=0, tiled=True)  31.1 us
    all_to_all x2, starting transfers between devices, exchanged(): return lax.all_to_all(value, axes, split_axis=0, concat_axis=0, tiled=True)  14.9 us
    pallas_call x3, Pallas kernels, pack(): pl.pallas_call(lambda *refs: pack_body(*refs, with_mask=mask is not None)...  9.16 us
    pallas_call x2, Pallas kernels, unpack(): pl.pallas_call(lambda *refs: unpack_body(*refs), grid=(1,), in_specs=[sma...  5.83 us
  transfers between devices with their start and end apart: 39, of which 12 were waited for; matrix products, arithmetic and copies ran while one was open for 1% of the time, Pallas kernels for 21%

profile of v1, /device:TPU:38, one launch (start us, length us, event | category | flops | bytes accessed | tf_op | source)
XLA Modules:
  0.0 179.5 jit_solution(4138825112332198579)
XLA Ops:
  1.5 15.1 %all_to_all.20 = bf16[8,24,96]{2,1,0:T(8,128)(2,1)S(1)} all-to-all(bf16[8,24,96]{2,1,0:T(8,128)(2,1)S(1)} %pad_maximum_fusion), channel_id=1, replica_groups=mesh['zh'=2,'x'=4,'y'=4,'z'=4,'core'=2] {'zh','z'}, dimensions={0} | all-to-all | bytes 73728 | tf_op jit(solution)/shard_map/all_to_all | solution.py:357
  16.8 16.0 %all_to_all.21.own = bf16[16,48,384]{2,1,0:T(8,128)(2,1)S(1)} all-to-all(bf16[16,48,384]{2,1,0:T(8,128)(2,1)S(1)} %broadcast_in_dim.3), channel_id=1, replica_groups=mesh['zh'=2,'x'=4,'y'=4,'z'=4,'core'=2] {'x','y'}, dimensions={0} | all-to-all | bytes 1179648 | tf_op jit(solution)/shard_map/all_to_all | solution.py:357
  33.4 3.1 %shard_map.96 = (bf16[384,128]{1,0:T(8,128)(2,1)}, bf16[384,128]{1,0:T(8,128)(2,1)}, bf16[384,128]{1,0:T(8,128)(2,1)}, bf16[384,128]{1,0:T(8,128)(2,1)}, bf16[38...) custom-call(s32[2]{0:T(128)} %pad_add_fusion.refs_0_.place, ...), custom_call_target="tpu_custom_call" | custom-call | flops 1000000000 | bytes 2000000 | tf_op jit(solution)/shard_map/pallas_call | solution.py:91
  38.5 3.0 %shard_map.94 = (bf16[400,128]{1,0:T(8,128)(2,1)}, bf16[400,128]{1,0:T(8,128)(2,1)}, bf16[400,128]{1,0:T(8,128)(2,1)}, bf16[400,128]{1,0:T(8,128)(2,1)}, bf16[40...) custom-call(s32[2]{0:T(128)} %pad_add_fusion.refs_0_.place, ...), custom_call_target="tpu_custom_call" | custom-call | flops 1000000000 | bytes 2000000 | tf_op jit(solution)/shard_map/pallas_call | solution.py:91
  43.6 2.4 %collective-permute-start.18 = (bf16[384,128]{1,0:T(8,128)(2,1)S(1)}, bf16[384,128]{1,0:T(8,128)(2,1)S(1)}, u32[]{:S(2)}, u32[]{:S(2)}) collective-permute-start(bf16[384,128]{1,0:T(8,128)(2,1)S(1)} %copy-done.30), channel_id=1, source_target_pairs={{0,4},{1,5},{2,6},{3,7},{4,0},{5,1},{6,2},{7,3},{8,12},{9,13},{10,... | collective-permute-start | bytes 294920 | tf_op jit(solution)/shard_map/ppermute | solution.py:345
  46.1 5.3 %collective-permute-done.17.refs_4_ = bf16[384,128]{1,0:T(8,128)(2,1)S(1)} collective-permute-done((bf16[384,128]{1,0:T(8,128)(2,1)S(1)}, bf16[384,128]{1,0:T(8,128)(2,1)S(1)}, u32[]{:S(2)}, u32[]{:S(2)}) %collective-permute-start.17) | collective-permute-done | bytes 98336 | tf_op jit(solution)/shard_map/ppermute | solution.py:345
  51.4 2.3 %collective-permute-start.12 = (bf16[400,128]{1,0:T(8,128)(2,1)}, bf16[400,128]{1,0:T(8,128)(2,1)S(1)}, u32[]{:S(2)}, u32[]{:S(2)}) collective-permute-start(bf16[400,128]{1,0:T(8,128)(2,1)} %get-tuple-element.77), channel_id=1, source_target_pairs={{0,5},{1,4},{2,7},{3,6},{4,1},{5,0},{6,3},{7,2},{8,13},{9,12},{10,... | collective-permute-start | bytes 307208 | tf_op jit(solution)/shard_map/ppermute | solution.py:345
  55.8 4.4 %collective-permute-start.9 = (bf16[400,128]{1,0:T(8,128)(2,1)}, bf16[400,128]{1,0:T(8,128)(2,1)S(1)}, u32[]{:S(2)}, u32[]{:S(2)}) collective-permute-start(bf16[400,128]{1,0:T(8,128)(2,1)} %get-tuple-element.74), channel_id=1, source_target_pairs={{0,2},{1,3},{2,0},{3,1},{4,6},{5,7},{6,4},{7,5},{8,10},{9,11},{10,... | collective-permute-start | bytes 307208 | tf_op jit(solution)/shard_map/ppermute | solution.py:345
  60.3 3.0 %shard_map.93 = (bf16[384,128]{1,0:T(8,128)(2,1)}, bf16[384,128]{1,0:T(8,128)(2,1)}, bf16[384,128]{1,0:T(8,128)(2,1)}, bf16[384,128]{1,0:T(8,128)(2,1)}, bf16[38...) custom-call(s32[2]{0:T(128)} %pad_add_fusion.refs_0_.place, ...), custom_call_target="tpu_custom_call" | custom-call | flops 1000000000 | bytes 2000000 | tf_op jit(solution)/shard_map/pallas_call | solution.py:91
  64.2 1.5 collective-permute-done.13.refs_7_
  66.2 1.9 %collective-permute-done.14.refs_8_ = bf16[400,128]{1,0:T(8,128)(2,1)S(1)} collective-permute-done((bf16[400,128]{1,0:T(8,128)(2,1)}, bf16[400,128]{1,0:T(8,128)(2,1)S(1)}, u32[]{:S(2)}, u32[]{:S(2)}) %collective-permute-start.14) | collective-permute-done | bytes 102432 | tf_op jit(solution)/shard_map/ppermute | solution.py:345
  68.2 1.8 %collective-permute-start.21 = (bf16[384,128]{1,0:T(8,128)(2,1)S(1)}, bf16[384,128]{1,0:T(8,128)(2,1)S(1)}, u32[]{:S(2)}, u32[]{:S(2)}) collective-permute-start(bf16[384,128]{1,0:T(8,128)(2,1)S(1)} %copy-done.20), channel_id=1, source_target_pairs={{0,7},{1,6},{2,5},{3,4},{4,3},{5,2},{6,1},{7,0},{8,15},{9,14},{10,... | collective-permute-start | bytes 294920 | tf_op jit(solution)/shard_map/ppermute | solution.py:345
  70.3 10.6 %shard_map.95 = (bf16[288,128]{1,0:T(8,128)(2,1)S(1)}, bf16[288,128]{1,0:T(8,128)(2,1)S(1)}, bf16[288,128]{1,0:T(8,128)(2,1)S(1)}, bf16[288,128]{1,0:T(8,128)(2,...) custom-call(s32[3]{0:T(128)S(1)} %pad_add_fusion.1.refs_0_, ...), custom_call_target="tpu_custom_call" | custom-call | flops 10000000000 | bytes 6000000 | tf_op jit(solution)/shard_map/pallas_call | solution.py:250
  81.0 1.6 collective-permute-start.2
  83.1 2.3 %collective-permute-start.4 = (bf16[384,128]{1,0:T(8,128)(2,1)S(1)}, bf16[384,128]{1,0:T(8,128)(2,1)S(1)}, u32[]{:S(2)}, u32[]{:S(2)}) collective-permute-start(bf16[384,128]{1,0:T(8,128)(2,1)S(1)} %copy-done.25), channel_id=1, source_target_pairs={{0,5},{1,4},{2,7},{3,6},{4,1},{5,0},{6,3},{7,2},{8,13},{9,12},{10,... | collective-permute-start | bytes 294920 | tf_op jit(solution)/shard_map/ppermute | solution.py:345
  87.0 10.5 %shard_map.97 = (bf16[576,128]{1,0:T(8,128)(2,1)S(1)}, bf16[576,128]{1,0:T(8,128)(2,1)S(1)}, bf16[576,128]{1,0:T(8,128)(2,1)S(1)}, bf16[576,128]{1,0:T(8,128)(2,...) custom-call(s32[3]{0:T(128)S(1)} %pad_add_fusion.1.refs_0_, ...), custom_call_target="tpu_custom_call", output_to_operand_aliasing={{8}: (19, {})} | custom-call | flops 10000000000 | bytes 6000000 | tf_op jit(solution)/shard_map/pallas_call | solution.py:250
  97.6 3.0 %collective-permute-done.5.refs_7_ = bf16[384,128]{1,0:T(8,128)(2,1)S(1)} collective-permute-done((bf16[384,128]{1,0:T(8,128)(2,1)S(1)}, bf16[384,128]{1,0:T(8,128)(2,1)S(1)}, u32[]{:S(2)}, u32[]{:S(2)}) %collective-permute-start.5) | collective-permute-done | bytes 98336 | tf_op jit(solution)/shard_map/ppermute | solution.py:345
  101.5 10.5 %shard_map.98 = (bf16[288,128]{1,0:T(8,128)(2,1)S(1)}, bf16[288,128]{1,0:T(8,128)(2,1)S(1)}, bf16[288,128]{1,0:T(8,128)(2,1)S(1)}, bf16[288,128]{1,0:T(8,128)(2,...) custom-call(s32[3]{0:T(128)S(1)} %pad_add_fusion.1.refs_0_, ...), custom_call_target="tpu_custom_call", output_to_operand_aliasing={{8}: (11, {})} | custom-call | flops 10000000000 | bytes 6000000 | tf_op jit(solution)/shard_map/pallas_call | solution.py:250
  113.5 1.6 collective-permute-done.36
  116.1 5.6 %all-to-all-start.2 = ((bf16[16,48,384]{2,1,0:T(8,128)(2,1)}), bf16[16,48,384]{2,1,0:T(8,128)(2,1)S(1)}, u32[]{:S(2)}, u32[]{:S(2)}) async-start(bf16[16,48,384]{2,1,0:T(8,128)(2,1)} %add_convert_fusion), calls=%async_computation.2 | async-start | bytes 1179648 | tf_op jit(solution)/shard_map/all_to_all | solution.py:357
  122.2 1.7 collective-permute-start.23
  123.9 2.3 %collective-permute-start.32 = (bf16[576,128]{1,0:T(8,128)(2,1)S(1)}, bf16[576,128]{1,0:T(8,128)(2,1)S(1)}, u32[]{:S(2)}, u32[]{:S(2)}) collective-permute-start(bf16[576,128]{1,0:T(8,128)(2,1)S(1)} %get-tuple-element.111), channel_id=1, source_target_pairs={{0,4},{1,5},{2,6},{3,7},{4,0},{5,1},{6,2},{7,3},{8,12},{9,13},{10,... | collective-permute-start | bytes 442376 | tf_op jit(solution)/shard_map/ppermute | solution.py:345
  126.2 4.4 %collective-permute-done.23.refs_3_ = bf16[288,128]{1,0:T(8,128)(2,1)S(1)} collective-permute-done((bf16[288,128]{1,0:T(8,128)(2,1)S(1)}, bf16[288,128]{1,0:T(8,128)(2,1)S(1)}, u32[]{:S(2)}, u32[]{:S(2)}) %collective-permute-start.23) | collective-permute-done | bytes 73760 | tf_op jit(solution)/shard_map/ppermute | solution.py:345
  131.8 3.4 %collective-permute-start.35 = (bf16[576,128]{1,0:T(8,128)(2,1)S(1)}, bf16[576,128]{1,0:T(8,128)(2,1)S(1)}, u32[]{:S(2)}, u32[]{:S(2)}) collective-permute-start(bf16[576,128]{1,0:T(8,128)(2,1)S(1)} %get-tuple-element.114), channel_id=1, source_target_pairs={{0,7},{1,6},{2,5},{3,4},{4,3},{5,2},{6,1},{7,0},{8,15},{9,14},{10,... | collective-permute-start | bytes 442376 | tf_op jit(solution)/shard_map/ppermute | solution.py:345
  135.2 1.6 collective-permute-start.24
  137.0 11.4 %collective-permute-done.33.refs_6_ = bf16[576,128]{1,0:T(8,128)(2,1)S(1)} collective-permute-done((bf16[576,128]{1,0:T(8,128)(2,1)S(1)}, bf16[576,128]{1,0:T(8,128)(2,1)S(1)}, u32[]{:S(2)}, u32[]{:S(2)}) %collective-permute-start.33) | collective-permute-done | bytes 147488 | tf_op jit(solution)/shard_map/ppermute | solution.py:345
  148.5 3.1 %collective-permute-start.26 = (bf16[288,128]{1,0:T(8,128)(2,1)S(1)}, bf16[288,128]{1,0:T(8,128)(2,1)S(1)}, u32[]{:S(2)}, u32[]{:S(2)}) collective-permute-start(bf16[288,128]{1,0:T(8,128)(2,1)S(1)} %get-tuple-element.104), channel_id=1, source_target_pairs={{0,5},{1,4},{2,7},{3,6},{4,1},{5,0},{6,3},{7,2},{8,13},{9,12},{10,... | collective-permute-start | bytes 221192 | tf_op jit(solution)/shard_map/ppermute | solution.py:345
  151.6 2.4 %collective-permute-done.34.refs_7_ = bf16[576,128]{1,0:T(8,128)(2,1)S(1)} collective-permute-done((bf16[576,128]{1,0:T(8,128)(2,1)S(1)}, bf16[576,128]{1,0:T(8,128)(2,1)S(1)}, u32[]{:S(2)}, u32[]{:S(2)}) %collective-permute-start.34) | collective-permute-done | bytes 147488 | tf_op jit(solution)/shard_map/ppermute | solution.py:345
  154.9 6.9 %collective-permute-done.35.refs_8_ = bf16[576,128]{1,0:T(8,128)(2,1)S(1)} collective-permute-done((bf16[576,128]{1,0:T(8,128)(2,1)S(1)}, bf16[576,128]{1,0:T(8,128)(2,1)S(1)}, u32[]{:S(2)}, u32[]{:S(2)}) %collective-permute-start.35) | collective-permute-done | bytes 147488 | tf_op jit(solution)/shard_map/ppermute | solution.py:345
  162.6 9.3 %all-to-all-start.3 = ((bf16[8,24,96]{2,1,0:T(8,128)(2,1)}), bf16[8,24,96]{2,1,0:T(8,128)(2,1)S(1)}, u32[]{:S(2)}, u32[]{:S(2)}) async-start(bf16[8,24,96]{2,1,0:T(8,128)(2,1)} %bitcast.13), calls=%async_computation.3 | async-start | bytes 98304 | tf_op jit(solution)/shard_map/all_to_all | solution.py:357
  172.0 3.3 %shard_map.99 = (bf16[2,12,96,128]{3,2,1,0:T(8,128)(2,1)}, bf16[2,12,96,128]{3,2,1,0:T(8,128)(2,1)}, bf16[2,12,96,128]{3,2,1,0:T(8,128)(2,1)}) custom-call(s32[2]{0:T(128)} %pad_add_fusion.refs_0_.place, bf16[576,128]{1,0:T(8,128)(2,1)} %copy-done, bf16[576,128]{1,0:T(8,128)(2,1)} %copy-done.6, bf16[576,128]{1,0:T(8,128)(2,1)} %copy-done.7, ...), custom_call_target="tpu_custom_call" | custom-call | tf_op jit(solution)/shard_map/pallas_call | solution.py:305
  176.1 2.5 %shard_map.100 = (bf16[2,12,96,128]{3,2,1,0:T(8,128)(2,1)}, bf16[2,12,96,128]{3,2,1,0:T(8,128)(2,1)}, bf16[2,12,96,128]{3,2,1,0:T(8,128)(2,1)}) custom-call(s32[2]{0:T(128)} %pad_add_fusion.refs_0_.place, bf16[288,128]{1,0:T(8,128)(2,1)} %copy-done.1, bf16[288,128]{1,0:T(8,128)(2,1)} %copy-done.13, ...), custom_call_target="tpu_custom_call", output_to_operand_aliasing={{0}: (9, {}), {1}: (10, {}), {2}: (11, {})} | custom-call | tf_op jit(solution)/shard_map/pallas_call | solution.py:305
  (133 shorter events, 20.3 us)
Async XLA Ops:
  32.8 23.1 %collective-permute-start.7 = (bf16[16,48,384]{2,1,0:T(8,128)(2,1)S(1)}, bf16[16,48,384]{2,1,0:T(8,128)(2,1)S(1)}, u32[]{:S(2)}, u32[]{:S(2)}) collective-permute-start(bf16[16,48,384]{2,1,0:T(8,128)(2,1)S(1)} %all_to_all.21.own), channel_id=1, source_target_pairs={{0,1},{1,0},{2,3},{3,2},{4,5},{5,4},{6,7},{7,6},{8,9},{9,8},{10,11... | collective-permute-start | bytes 1769480 | tf_op jit(solution)/shard_map/ppermute | solution.py:345
  41.6 13.4 %collective-permute-start.10 = (bf16[400,128]{1,0:T(8,128)(2,1)}, bf16[400,128]{1,0:T(8,128)(2,1)S(1)}, u32[]{:S(2)}, u32[]{:S(2)}) collective-permute-start(bf16[400,128]{1,0:T(8,128)(2,1)} %get-tuple-element.75), channel_id=1, source_target_pairs={{0,3},{1,2},{2,1},{3,0},{4,7},{5,6},{6,5},{7,4},{8,11},{9,10},{10,... | collective-permute-start | bytes 307208 | tf_op jit(solution)/shard_map/ppermute | solution.py:345
  41.7 13.8 %collective-permute-start.11 = (bf16[400,128]{1,0:T(8,128)(2,1)}, bf16[400,128]{1,0:T(8,128)(2,1)S(1)}, u32[]{:S(2)}, u32[]{:S(2)}) collective-permute-start(bf16[400,128]{1,0:T(8,128)(2,1)} %get-tuple-element.76), channel_id=1, source_target_pairs={{0,4},{1,5},{2,6},{3,7},{4,0},{5,1},{6,2},{7,3},{8,12},{9,13},{10,... | collective-permute-start | bytes 307208 | tf_op jit(solution)/shard_map/ppermute | solution.py:345
  43.6 10.0 %collective-permute-start.18 = (bf16[384,128]{1,0:T(8,128)(2,1)S(1)}, bf16[384,128]{1,0:T(8,128)(2,1)S(1)}, u32[]{:S(2)}, u32[]{:S(2)}) collective-permute-start(bf16[384,128]{1,0:T(8,128)(2,1)S(1)} %copy-done.30), channel_id=1, source_target_pairs={{0,4},{1,5},{2,6},{3,7},{4,0},{5,1},{6,2},{7,3},{8,12},{9,13},{10,... | collective-permute-start | bytes 294920 | tf_op jit(solution)/shard_map/ppermute | solution.py:345
  51.4 12.7 %collective-permute-start.12 = (bf16[400,128]{1,0:T(8,128)(2,1)}, bf16[400,128]{1,0:T(8,128)(2,1)S(1)}, u32[]{:S(2)}, u32[]{:S(2)}) collective-permute-start(bf16[400,128]{1,0:T(8,128)(2,1)} %get-tuple-element.77), channel_id=1, source_target_pairs={{0,5},{1,4},{2,7},{3,6},{4,1},{5,0},{6,3},{7,2},{8,13},{9,12},{10,... | collective-permute-start | bytes 307208 | tf_op jit(solution)/shard_map/ppermute | solution.py:345
  53.7 12.1 %collective-permute-start.13 = (bf16[400,128]{1,0:T(8,128)(2,1)}, bf16[400,128]{1,0:T(8,128)(2,1)S(1)}, u32[]{:S(2)}, u32[]{:S(2)}) collective-permute-start(bf16[400,128]{1,0:T(8,128)(2,1)} %get-tuple-element.78), channel_id=1, source_target_pairs={{0,6},{1,7},{2,4},{3,5},{4,2},{5,3},{6,0},{7,1},{8,14},{9,15},{10,... | collective-permute-start | bytes 307208 | tf_op jit(solution)/shard_map/ppermute | solution.py:345
  55.0 13.2 %collective-permute-start.14 = (bf16[400,128]{1,0:T(8,128)(2,1)}, bf16[400,128]{1,0:T(8,128)(2,1)S(1)}, u32[]{:S(2)}, u32[]{:S(2)}) collective-permute-start(bf16[400,128]{1,0:T(8,128)(2,1)} %get-tuple-element.79), channel_id=1, source_target_pairs={{0,7},{1,6},{2,5},{3,4},{4,3},{5,2},{6,1},{7,0},{8,15},{9,14},{10,... | collective-permute-start | bytes 307208 | tf_op jit(solution)/shard_map/ppermute | solution.py:345
  55.4 14.5 %collective-permute-start.8 = (bf16[400,128]{1,0:T(8,128)(2,1)}, bf16[400,128]{1,0:T(8,128)(2,1)S(1)}, u32[]{:S(2)}, u32[]{:S(2)}) collective-permute-start(bf16[400,128]{1,0:T(8,128)(2,1)} %get-tuple-element.73), channel_id=1, source_target_pairs={{0,1},{1,0},{2,3},{3,2},{4,5},{5,4},{6,7},{7,6},{8,9},{9,8},{10,11... | collective-permute-start | bytes 307208 | tf_op jit(solution)/shard_map/ppermute | solution.py:345
  55.8 14.2 %collective-permute-start.9 = (bf16[400,128]{1,0:T(8,128)(2,1)}, bf16[400,128]{1,0:T(8,128)(2,1)S(1)}, u32[]{:S(2)}, u32[]{:S(2)}) collective-permute-start(bf16[400,128]{1,0:T(8,128)(2,1)} %get-tuple-element.74), channel_id=1, source_target_pairs={{0,2},{1,3},{2,0},{3,1},{4,6},{5,7},{6,4},{7,5},{8,10},{9,11},{10,... | collective-permute-start | bytes 307208 | tf_op jit(solution)/shard_map/ppermute | solution.py:345
  64.2 16.7 %collective-permute-start.19 = (bf16[384,128]{1,0:T(8,128)(2,1)S(1)}, bf16[384,128]{1,0:T(8,128)(2,1)S(1)}, u32[]{:S(2)}, u32[]{:S(2)}) collective-permute-start(bf16[384,128]{1,0:T(8,128)(2,1)S(1)} %copy-done.22), channel_id=1, source_target_pairs={{0,5},{1,4},{2,7},{3,6},{4,1},{5,0},{6,3},{7,2},{8,13},{9,12},{10,... | collective-permute-start | bytes 294920 | tf_op jit(solution)/shard_map/ppermute | solution.py:345
  65.8 16.8 %collective-permute-start.20 = (bf16[384,128]{1,0:T(8,128)(2,1)S(1)}, bf16[384,128]{1,0:T(8,128)(2,1)S(1)}, u32[]{:S(2)}, u32[]{:S(2)}) collective-permute-start(bf16[384,128]{1,0:T(8,128)(2,1)S(1)} %copy-done.21), channel_id=1, source_target_pairs={{0,6},{1,7},{2,4},{3,5},{4,2},{5,3},{6,0},{7,1},{8,14},{9,15},{10,... | collective-permute-start | bytes 294920 | tf_op jit(solution)/shard_map/ppermute | solution.py:345
  68.2 14.9 %collective-permute-start.21 = (bf16[384,128]{1,0:T(8,128)(2,1)S(1)}, bf16[384,128]{1,0:T(8,128)(2,1)S(1)}, u32[]{:S(2)}, u32[]{:S(2)}) collective-permute-start(bf16[384,128]{1,0:T(8,128)(2,1)S(1)} %copy-done.20), channel_id=1, source_target_pairs={{0,7},{1,6},{2,5},{3,4},{4,3},{5,2},{6,1},{7,0},{8,15},{9,14},{10,... | collective-permute-start | bytes 294920 | tf_op jit(solution)/shard_map/ppermute | solution.py:345
  70.0 15.5 %collective-permute-start = (bf16[384,128]{1,0:T(8,128)(2,1)S(1)}, bf16[384,128]{1,0:T(8,128)(2,1)S(1)}, u32[]{:S(2)}, u32[]{:S(2)}) collective-permute-start(bf16[384,128]{1,0:T(8,128)(2,1)S(1)} %copy-done.29), channel_id=1, source_target_pairs={{0,1},{1,0},{2,3},{3,2},{4,5},{5,4},{6,7},{7,6},{8,9},{9,8},{10,11... | collective-permute-start | bytes 294920 | tf_op jit(solution)/shard_map/ppermute | solution.py:345
  70.1 15.5 %collective-permute-start.1 = (bf16[384,128]{1,0:T(8,128)(2,1)S(1)}, bf16[384,128]{1,0:T(8,128)(2,1)S(1)}, u32[]{:S(2)}, u32[]{:S(2)}) collective-permute-start(bf16[384,128]{1,0:T(8,128)(2,1)S(1)} %copy-done.28), channel_id=1, source_target_pairs={{0,2},{1,3},{2,0},{3,1},{4,6},{5,7},{6,4},{7,5},{8,10},{9,11},{10,... | collective-permute-start | bytes 294920 | tf_op jit(solution)/shard_map/ppermute | solution.py:345
  81.0 16.6 %collective-permute-start.2 = (bf16[384,128]{1,0:T(8,128)(2,1)S(1)}, bf16[384,128]{1,0:T(8,128)(2,1)S(1)}, u32[]{:S(2)}, u32[]{:S(2)}) collective-permute-start(bf16[384,128]{1,0:T(8,128)(2,1)S(1)} %copy-done.27), channel_id=1, source_target_pairs={{0,3},{1,2},{2,1},{3,0},{4,7},{5,6},{6,5},{7,4},{8,11},{9,10},{10,... | collective-permute-start | bytes 294920 | tf_op jit(solution)/shard_map/ppermute | solution.py:345
  82.6 15.0 %collective-permute-start.3 = (bf16[384,128]{1,0:T(8,128)(2,1)S(1)}, bf16[384,128]{1,0:T(8,128)(2,1)S(1)}, u32[]{:S(2)}, u32[]{:S(2)}) collective-permute-start(bf16[384,128]{1,0:T(8,128)(2,1)S(1)} %copy-done.26), channel_id=1, source_target_pairs={{0,4},{1,5},{2,6},{3,7},{4,0},{5,1},{6,2},{7,3},{8,12},{9,13},{10,... | collective-permute-start | bytes 294920 | tf_op jit(solution)/shard_map/ppermute | solution.py:345
  83.1 14.5 %collective-permute-start.4 = (bf16[384,128]{1,0:T(8,128)(2,1)S(1)}, bf16[384,128]{1,0:T(8,128)(2,1)S(1)}, u32[]{:S(2)}, u32[]{:S(2)}) collective-permute-start(bf16[384,128]{1,0:T(8,128)(2,1)S(1)} %copy-done.25), channel_id=1, source_target_pairs={{0,5},{1,4},{2,7},{3,6},{4,1},{5,0},{6,3},{7,2},{8,13},{9,12},{10,... | collective-permute-start | bytes 294920 | tf_op jit(solution)/shard_map/ppermute | solution.py:345
  85.4 15.2 %collective-permute-start.5 = (bf16[384,128]{1,0:T(8,128)(2,1)S(1)}, bf16[384,128]{1,0:T(8,128)(2,1)S(1)}, u32[]{:S(2)}, u32[]{:S(2)}) collective-permute-start(bf16[384,128]{1,0:T(8,128)(2,1)S(1)} %copy-done.24), channel_id=1, source_target_pairs={{0,6},{1,7},{2,4},{3,5},{4,2},{5,3},{6,0},{7,1},{8,14},{9,15},{10,... | collective-permute-start | bytes 294920 | tf_op jit(solution)/shard_map/ppermute | solution.py:345
  85.6 15.9 %collective-permute-start.6 = (bf16[384,128]{1,0:T(8,128)(2,1)S(1)}, bf16[384,128]{1,0:T(8,128)(2,1)S(1)}, u32[]{:S(2)}, u32[]{:S(2)}) collective-permute-start(bf16[384,128]{1,0:T(8,128)(2,1)S(1)} %copy-done.23), channel_id=1, source_target_pairs={{0,7},{1,6},{2,5},{3,4},{4,3},{5,2},{6,1},{7,0},{8,15},{9,14},{10,... | collective-permute-start | bytes 294920 | tf_op jit(solution)/shard_map/ppermute | solution.py:345
  116.1 45.7 %all-to-all-start.2 = ((bf16[16,48,384]{2,1,0:T(8,128)(2,1)}), bf16[16,48,384]{2,1,0:T(8,128)(2,1)S(1)}, u32[]{:S(2)}, u32[]{:S(2)}) async-start(bf16[16,48,384]{2,1,0:T(8,128)(2,1)} %add_convert_fusion), calls=%async_computation.2 | async-start | bytes 1179648 | tf_op jit(solution)/shard_map/all_to_all | solution.py:357
  121.8 10.0 %collective-permute-start.30 = (bf16[576,128]{1,0:T(8,128)(2,1)S(1)}, bf16[576,128]{1,0:T(8,128)(2,1)S(1)}, u32[]{:S(2)}, u32[]{:S(2)}) collective-permute-start(bf16[576,128]{1,0:T(8,128)(2,1)S(1)} %get-tuple-element.109), channel_id=1, source_target_pairs={{0,2},{1,3},{2,0},{3,1},{4,6},{5,7},{6,4},{7,5},{8,10},{9,11},{10,... | collective-permute-start | bytes 442376 | tf_op jit(solution)/shard_map/ppermute | solution.py:345
  123.9 11.3 %collective-permute-start.31 = (bf16[576,128]{1,0:T(8,128)(2,1)S(1)}, bf16[576,128]{1,0:T(8,128)(2,1)S(1)}, u32[]{:S(2)}, u32[]{:S(2)}) collective-permute-start(bf16[576,128]{1,0:T(8,128)(2,1)S(1)} %get-tuple-element.110), channel_id=1, source_target_pairs={{0,3},{1,2},{2,1},{3,0},{4,7},{5,6},{6,5},{7,4},{8,11},{9,10},{10,... | collective-permute-start | bytes 442376 | tf_op jit(solution)/shard_map/ppermute | solution.py:345
  123.9 13.1 %collective-permute-start.32 = (bf16[576,128]{1,0:T(8,128)(2,1)S(1)}, bf16[576,128]{1,0:T(8,128)(2,1)S(1)}, u32[]{:S(2)}, u32[]{:S(2)}) collective-permute-start(bf16[576,128]{1,0:T(8,128)(2,1)S(1)} %get-tuple-element.111), channel_id=1, source_target_pairs={{0,4},{1,5},{2,6},{3,7},{4,0},{5,1},{6,2},{7,3},{8,12},{9,13},{10,... | collective-permute-start | bytes 442376 | tf_op jit(solution)/shard_map/ppermute | solution.py:345
  130.6 17.9 %collective-permute-start.33 = (bf16[576,128]{1,0:T(8,128)(2,1)S(1)}, bf16[576,128]{1,0:T(8,128)(2,1)S(1)}, u32[]{:S(2)}, u32[]{:S(2)}) collective-permute-start(bf16[576,128]{1,0:T(8,128)(2,1)S(1)} %get-tuple-element.112), channel_id=1, source_target_pairs={{0,5},{1,4},{2,7},{3,6},{4,1},{5,0},{6,3},{7,2},{8,13},{9,12},{10,... | collective-permute-start | bytes 442376 | tf_op jit(solution)/shard_map/ppermute | solution.py:345
  130.6 23.3 %collective-permute-start.34 = (bf16[576,128]{1,0:T(8,128)(2,1)S(1)}, bf16[576,128]{1,0:T(8,128)(2,1)S(1)}, u32[]{:S(2)}, u32[]{:S(2)}) collective-permute-start(bf16[576,128]{1,0:T(8,128)(2,1)S(1)} %get-tuple-element.113), channel_id=1, source_target_pairs={{0,6},{1,7},{2,4},{3,5},{4,2},{5,3},{6,0},{7,1},{8,14},{9,15},{10,... | collective-permute-start | bytes 442376 | tf_op jit(solution)/shard_map/ppermute | solution.py:345
  131.8 30.0 %collective-permute-start.35 = (bf16[576,128]{1,0:T(8,128)(2,1)S(1)}, bf16[576,128]{1,0:T(8,128)(2,1)S(1)}, u32[]{:S(2)}, u32[]{:S(2)}) collective-permute-start(bf16[576,128]{1,0:T(8,128)(2,1)S(1)} %get-tuple-element.114), channel_id=1, source_target_pairs={{0,7},{1,6},{2,5},{3,4},{4,3},{5,2},{6,1},{7,0},{8,15},{9,14},{10,... | collective-permute-start | bytes 442376 | tf_op jit(solution)/shard_map/ppermute | solution.py:345
  135.2 40.1 %collective-permute-start.24 = (bf16[288,128]{1,0:T(8,128)(2,1)S(1)}, bf16[288,128]{1,0:T(8,128)(2,1)S(1)}, u32[]{:S(2)}, u32[]{:S(2)}) collective-permute-start(bf16[288,128]{1,0:T(8,128)(2,1)S(1)} %get-tuple-element.102), channel_id=1, source_target_pairs={{0,3},{1,2},{2,1},{3,0},{4,7},{5,6},{6,5},{7,4},{8,11},{9,10},{10,... | collective-permute-start | bytes 221192 | tf_op jit(solution)/shard_map/ppermute | solution.py:345
  137.0 38.3 %collective-permute-start.25 = (bf16[288,128]{1,0:T(8,128)(2,1)S(1)}, bf16[288,128]{1,0:T(8,128)(2,1)S(1)}, u32[]{:S(2)}, u32[]{:S(2)}) collective-permute-start(bf16[288,128]{1,0:T(8,128)(2,1)S(1)} %get-tuple-element.103), channel_id=1, source_target_pairs={{0,4},{1,5},{2,6},{3,7},{4,0},{5,1},{6,2},{7,3},{8,12},{9,13},{10,... | collective-permute-start | bytes 221192 | tf_op jit(solution)/shard_map/ppermute | solution.py:345
  148.5 26.9 %collective-permute-start.26 = (bf16[288,128]{1,0:T(8,128)(2,1)S(1)}, bf16[288,128]{1,0:T(8,128)(2,1)S(1)}, u32[]{:S(2)}, u32[]{:S(2)}) collective-permute-start(bf16[288,128]{1,0:T(8,128)(2,1)S(1)} %get-tuple-element.104), channel_id=1, source_target_pairs={{0,5},{1,4},{2,7},{3,6},{4,1},{5,0},{6,3},{7,2},{8,13},{9,12},{10,... | collective-permute-start | bytes 221192 | tf_op jit(solution)/shard_map/ppermute | solution.py:345
  154.0 21.4 %collective-permute-start.27 = (bf16[288,128]{1,0:T(8,128)(2,1)S(1)}, bf16[288,128]{1,0:T(8,128)(2,1)S(1)}, u32[]{:S(2)}, u32[]{:S(2)}) collective-permute-start(bf16[288,128]{1,0:T(8,128)(2,1)S(1)} %get-tuple-element.105), channel_id=1, source_target_pairs={{0,6},{1,7},{2,4},{3,5},{4,2},{5,3},{6,0},{7,1},{8,14},{9,15},{10,... | collective-permute-start | bytes 221192 | tf_op jit(solution)/shard_map/ppermute | solution.py:345
  161.8 13.6 %collective-permute-start.28 = (bf16[288,128]{1,0:T(8,128)(2,1)S(1)}, bf16[288,128]{1,0:T(8,128)(2,1)S(1)}, u32[]{:S(2)}, u32[]{:S(2)}) collective-permute-start(bf16[288,128]{1,0:T(8,128)(2,1)S(1)} %get-tuple-element.106), channel_id=1, source_target_pairs={{0,7},{1,6},{2,5},{3,4},{4,3},{5,2},{6,1},{7,0},{8,15},{9,14},{10,... | collective-permute-start | bytes 221192 | tf_op jit(solution)/shard_map/ppermute | solution.py:345
  162.6 16.3 %all-to-all-start.3 = ((bf16[8,24,96]{2,1,0:T(8,128)(2,1)}), bf16[8,24,96]{2,1,0:T(8,128)(2,1)S(1)}, u32[]{:S(2)}, u32[]{:S(2)}) async-start(bf16[8,24,96]{2,1,0:T(8,128)(2,1)} %bitcast.13), calls=%async_computation.3 | async-start | bytes 98304 | tf_op jit(solution)/shard_map/all_to_all | solution.py:357
  (39 other events, 523.1 us)
